TPU v7x, 32 devices: a 4x4x1 block of a 4x4x8 slice. The times are simulated.
32 devices in a mesh: dp: 1 (over z), tp2: 4 (over y), tp: 8 (over x, core).
Axes of the slice: x: 4, y: 4, z: 1, core: 2. Of those that a mesh axis runs over, the one named last changes fastest.
The devices are a block of a 4x4x8 slice.
Arguments:
- hidden: bfloat16 [512, 2304], P('dp')
- w_gate: bfloat16 [2304, 9216], P(None, ('tp2', 'tp'))
- w_up: bfloat16 [2304, 9216], P(None, ('tp2', 'tp'))
- w_down: bfloat16 [9216, 2304], P(('tp2', 'tp'))
- norm_gain: float32 [2304], replicated
- w_vocab: bfloat16 [2304, 256000], P(None, ('tp2', 'tp'))
- temperature: float32 [512], P('dp')
- target_ids: int32 [512], P('dp')
Outputs:
- output 1: float32 [512], P('dp')
- output 2: float32 [512], P('dp')
- output 3: float32 [512], P('dp')
- output 4: bfloat16 [512, 256000], P('dp', ('tp2', 'tp'))
All inputs are finite; a program needn't handle non-finite values.
Results may differ from a plain program's by a relative error of at most 0.00381759.
Values are sent between devices in bfloat16 or wider.
A program may use at most 768 MiB of HBM per device.

v0:
```python
import jax
import jax.numpy as jnp
from jax import lax
from jax.sharding import PartitionSpec as P

NORM_EPS = 1e-6


def solution(mesh):
    model_axes = ('tp2', 'tp')
    tp_size = mesh.shape['tp']

    def local_step(hidden, w_gate, w_up, w_down, norm_gain, w_vocab, value_a11, target_ids):
        gate_pre = jnp.dot(hidden, w_gate, preferred_element_type=jnp.float32)
        up_pre = jnp.dot(hidden, w_up, preferred_element_type=jnp.float32)
        hidden_act = (jax.nn.silu(gate_pre) * up_pre).astype(jnp.bfloat16)
        part_out = jnp.dot(hidden_act, w_down, preferred_element_type=jnp.float32).astype(jnp.bfloat16)
        mlp_out = lax.psum(part_out, model_axes)
        resid_sum = hidden.astype(jnp.float32) + mlp_out.astype(jnp.float32)
        inv_rms = lax.rsqrt(jnp.mean(resid_sum * resid_sum, axis=-1, keepdims=True) + NORM_EPS)
        normed = (norm_gain * resid_sum * inv_rms).astype(jnp.bfloat16)
        logits = jnp.dot(normed, w_vocab, preferred_element_type=jnp.float32) / value_a11[:, None]
        shard_cols = logits.shape[1]
        shard_index = lax.axis_index('tp2') * tp_size + lax.axis_index('tp')
        local_max = jnp.max(logits, axis=-1)
        shifted = jnp.exp(logits - local_max[:, None])
        local_sum = jnp.sum(shifted, axis=-1)
        local_moment = jnp.sum(shifted * logits, axis=-1)
        local_ids = target_ids - shard_index * shard_cols
        col_ids = jnp.arange(shard_cols, dtype=jnp.int32)
        local_target = jnp.sum(jnp.where(col_ids[None, :] == local_ids[:, None], logits, 0.0), axis=-1)
        global_max = lax.pmax(local_max, model_axes)
        rescale = jnp.exp(local_max - global_max)
        row_stats = jnp.stack([local_sum * rescale, local_moment * rescale, local_target], axis=0)
        totals = lax.psum(row_stats, model_axes)
        log_norm = global_max + jnp.log(totals[0])
        entropy = log_norm - totals[1] / totals[0]
        target_logp = totals[2] - log_norm
        logprobs = (logits - log_norm[:, None]).astype(jnp.bfloat16)
        return log_norm, entropy, target_logp, logprobs

    return jax.shard_map(
        local_step, mesh=mesh,
        in_specs=(P('dp', None), P(None, model_axes), P(None, model_axes), P(model_axes, None),
                  P(None), P(None, model_axes), P('dp'), P('dp')),
        out_specs=(P('dp'), P('dp'), P('dp'), P('dp', model_axes)),
        check_vma=False)
```

profile of v0, /device:TPU:97, one launch (start us, length us, event | category | flops | bytes accessed | tf_op | source)
XLA Modules:
  0.0 263.4 jit_solution(7797937322652963821)
XLA Ops:
  7.2 0.0 copy-start
  7.2 0.0 copy-start.6
  7.2 0.1 all-reduce.2.cloned.1.call-start
  7.3 3.1 %fusion.15 = f32[512,288]{0,1:T(8,128)S(1)} fusion(bf16[512,2304]{1,0:T(8,128)(2,1)} %param.8, bf16[2304,288]{0,1:T(8,128)(2,1)} %param.9), kind=kOutput, calls=%fused_computation.32 | convolution fusion | flops 679477248 | bytes 4276224 | tf_op jit(solution)/shard_map/dot_general | solution.py:14
  10.3 0.0 copy-done
  10.3 0.0 copy-done.6
  10.4 0.0 copy-start.5
  10.4 5.4 %convolution_convert_fusion = bf16[512,2304]{1,0:T(8,128)(2,1)} fusion(bf16[288,2304]{1,0:T(8,128)(2,1)S(1)} %copy-done, bf16[512,2304]{1,0:T(8,128)(2,1)} %param.8, bf16[2304,288]{0,1:T(8,128)(2,1)S(1)} %copy-done.6, f32[512,288]{0,1:T(8,128)S(1)} %fusion.15), kind=kOutput, calls=%fused_computation.10 | convolution fusion | flops 1361018880 | bytes 7962624 | tf_op jit(solution)/shard_map/dot_general | solution.py:17
  15.8 0.0 copy-start.7
  15.8 0.0 copy-start.8
  15.8 0.1 all-reduce.2.cloned.1.call-update
  15.8 0.0 copy-done.5
  15.9 101.7 %all-reduce.2.cloned.1.call-done = bf16[512,2304]{1,0:T(8,128)(2,1)} async-done(((bf16[512,2304]{1,0:T(8,128)(2,1)}), bf16[512,2304]{1,0:T(8,128)(2,1)}) %all-reduce.2.cloned.1.call-update) | async-done | bytes 2359312 | tf_op jit(solution)/shard_map/psum | solution.py:18
  117.6 0.0 copy-start.2
  117.6 0.0 copy-start.3
  117.6 3.4 %multiply_reduce_fusion.1 = f32[512]{0:T(512)S(1)} fusion(bf16[512,2304]{1,0:T(8,128)(2,1)} %all-reduce.2.cloned.1.call-done, bf16[512,2304]{1,0:T(8,128)(2,1)} %param.8), kind=kLoop, calls=%fused_computation.8 | loop fusion | flops 5897728 | bytes 4720640 | tf_op jit(solution)/shard_map/reduce_sum | solution.py:20
  120.9 0.0 copy-done.7
  121.0 0.0 copy-done.8
  121.0 0.0 copy-done.2
  121.0 0.4 copy-done.3
  121.4 27.4 %fusion.14 = (f32[512]{0:T(512)S(1)}, f32[512,8000]{0,1:T(8,128)}) fusion(f32[512]{0:T(512)S(1)} %copy-done.8, bf16[2304,8000]{0,1:T(8,128)(2,1)} %param.13, bf16[512,2304]{1,0:T(8,128)(2,1)S(1)} %copy-done.3, bf16[512,2304]{1,0:T(8,128)(2,1)S(1)} %copy-done.2, f32[512]{0:T(512)S(1)} %add_rsqrt_fusion, f32[2304]{0:T(1024)S(1)} %copy-done.7), kind=kOutput, calls=%fused_computation.31 | convolution fusion | flops 18889637888 | bytes 57981952 | tf_op jit(solution)/shard_map/dot_general | solution.py:22
  148.7 45.6 %pmax.7 = f32[512]{0:T(512)S(1)} all-reduce(f32[512]{0:T(512)S(1)} %get-tuple-element.14), channel_id=1, replica_groups=mesh['dp'=1,'tp2'=4,'tp'=8] {'tp2','tp'}, use_global_device_ids=true, to_apply=%region_3.4 | all-reduce | flops 512 | bytes 4096 | tf_op jit(solution)/shard_map/pmax | solution.py:32
  194.3 8.5 %fusion = (f32[512]{0:T(512)S(1)}, f32[512]{0:T(512)S(1)}, f32[512]{0:T(512)S(1)}) fusion(f32[512,8000]{0,1:T(8,128)} %get-tuple-element.15, f32[512]{0:T(512)S(1)} %get-tuple-element.14, s32[512]{0:T(512)S(1)} %broadcast_subtract_fusion), kind=kLoop, calls=%fused_computation.5 | loop fusion | flops 28670464 | bytes 16394240 | tf_op jit(solution)/shard_map/reduce_sum | solution.py:27
  202.9 43.6 %psum.15 = f32[3,512]{1,0:T(4,128)S(1)} all-reduce(f32[3,512]{1,0:T(4,128)S(1)} %pad_maximum_fusion), channel_id=1, replica_groups=mesh['dp'=1,'tp2'=4,'tp'=8] {'tp2','tp'}, use_global_device_ids=true, to_apply=%region_7.8 | all-reduce | flops 1536 | bytes 12288 | tf_op jit(solution)/shard_map/psum | solution.py:35
  246.5 0.6 fusion.13
  247.1 0.0 copy-start.4
  247.1 0.0 copy-start.1
  247.1 8.9 %subtract_convert_fusion = bf16[512,8000]{0,1:T(8,128)(2,1)} fusion(f32[512,8000]{0,1:T(8,128)} %get-tuple-element.15, f32[512]{0:T(512)S(1)} %get-tuple-element.8), kind=kLoop, calls=%fused_computation | loop fusion | flops 8192000 | bytes 24578048 | tf_op jit(solution)/shard_map/convert_element_type | solution.py:39
  256.0 0.0 copy-done.4
  256.0 0.6 sub.36
  256.6 0.0 copy-done.1
  (5 shorter events, 0.0 us)
Async XLA Ops:
  7.2 3.2 %copy-start = (bf16[288,2304]{1,0:T(8,128)(2,1)S(1)}, bf16[288,2304]{1,0:T(8,128)(2,1)}, u32[]{:S(2)}) copy-start(bf16[288,2304]{1,0:T(8,128)(2,1)} %param.11) | copy-start | bytes 3981316
  7.2 3.2 %copy-start.6 = (bf16[2304,288]{0,1:T(8,128)(2,1)S(1)}, bf16[2304,288]{0,1:T(8,128)(2,1)}, u32[]{:S(2)}) copy-start(bf16[2304,288]{0,1:T(8,128)(2,1)} %param.10) | copy-start | bytes 3981316
  7.2 110.4 %all-reduce.2.cloned.1.call-start = ((), (), s32[]{:S(2)}) async-start(), calls=%async_computation | async-start | bytes 4718592 | tf_op jit(solution)/shard_map/psum | solution.py:18
  10.4 5.5 %copy-start.5 = (s32[512]{0:T(512)S(1)}, s32[512]{0:T(512)}, u32[]{:S(2)}) copy-start(s32[512]{0:T(512)} %param.15) | copy-start | bytes 6148
  15.8 105.2 %copy-start.7 = (f32[2304]{0:T(1024)S(1)}, f32[2304]{0:T(1024)}, u32[]{:S(2)}) copy-start(f32[2304]{0:T(1024)} %param.12) | copy-start | bytes 27652
  15.8 105.2 %copy-start.8 = (f32[512]{0:T(512)S(1)}, f32[512]{0:T(512)}, u32[]{:S(2)}) copy-start(f32[512]{0:T(512)} %param.14) | copy-start | bytes 6148
  117.6 3.4 %copy-start.2 = (bf16[512,2304]{1,0:T(8,128)(2,1)S(1)}, bf16[512,2304]{1,0:T(8,128)(2,1)}, u32[]{:S(2)}) copy-start(bf16[512,2304]{1,0:T(8,128)(2,1)} %param.8) | copy-start | bytes 7077892
  117.6 3.8 %copy-start.3 = (bf16[512,2304]{1,0:T(8,128)(2,1)S(1)}, bf16[512,2304]{1,0:T(8,128)(2,1)}, u32[]{:S(2)}) copy-start(bf16[512,2304]{1,0:T(8,128)(2,1)} %all-reduce.2.cloned.1.call-done) | copy-start | bytes 7077892
  247.1 8.9 %copy-start.4 = (f32[512]{0:T(512)}, f32[512]{0:T(512)S(1)}, u32[]{:S(2)}) copy-start(f32[512]{0:T(512)S(1)} %get-tuple-element.8) | copy-start | bytes 6148
  247.1 9.5 %copy-start.1 = (bf16[288,2304]{1,0:T(8,128)(2,1)S(1)}, bf16[288,2304]{1,0:T(8,128)(2,1)}, u32[]{:S(2)}) copy-start(bf16[288,2304]{1,0:T(8,128)(2,1)} %param.11) | copy-start | bytes 3981316
Sparse Core Ops, SparseCore 0:
  15.9 101.5 all-reduce.1
where the time goes:
time: 264 us; the launch traced here: 263 us
  waiting for transfers between devices  102 us (39%)
  blocking collectives  89.2 us (34%)
  matrix products  35.8 us (14%)
  other arithmetic  22 us (8%)
  between operations  14.2 us (5%)
    psum x1, waiting for transfers between devices, local_step(): mlp_out = lax.psum(part_out, model_axes)  102 us
    pmax x1, blocking collectives, local_step(): global_max = lax.pmax(local_max, model_axes)  45.6 us
    psum x1, blocking collectives, local_step(): totals = lax.psum(row_stats, model_axes)  43.6 us
    dot_general x1, matrix products, local_step(): jnp.dot(normed, w_vocab, preferred_element_type=jnp.float32)  27.4 us
    convert_element_type x1, other arithmetic, local_step(): logprobs = (logits - log_norm[:, None]).astype(jnp.bfloat16)  8.88 us
    reduce_sum x1, other arithmetic, local_step(): local_sum = jnp.sum(shifted, axis=-1)  8.54 us
    dot_general x1, matrix products, local_step(): jnp.dot(hidden_act, w_down, preferred_element_type=jnp.float32)  5.39 us
  transfers between devices with their start and end apart: 1, of which 1 were waited for; matrix products, arithmetic and copies ran while one was open for 0% of the time, Pallas kernels for 0%

commit v1 on v0

v1 whole, which is shorter than its diff:
```python
import jax
import jax.numpy as jnp
from jax import lax
from jax.experimental import pallas as pl
from jax.experimental.pallas import tpu as pltpu
from jax.sharding import PartitionSpec as P

NORM_EPS = 1e-6
CORES = 2
CHUNKS = 2
BLOCKS = 10
MESH = pl.DeviceIdType.MESH
NT = (((1,), (1,)), ((), ()))
F32, BF16 = jnp.float32, jnp.bfloat16


def split(start, stop, pieces):
    step = -(-(stop - start) // pieces)
    step = -(-step // 16) * 16
    return [(i, min(step, stop - i)) for i in range(start, stop, step)]


def main_kernel(n2, n1, hid, hid3, wg, wu, wd, gain, wvt, temp, tid, lg, stats,
                wv, yp, d0, st1, st2, xf, xm, hs, act, so, sr,
                load_sem, hs_sem, s0_s, s0_r, s1_s, s1_r, s2_s, s2_r,
                ga_s, gb_s, gc_s, g_r, so_s, so_r):
    group = n1 * n2
    half = group // CORES
    rows, width = hid.shape
    ff = wg.shape[0]
    vocab = wvt.shape[0]
    chunk = rows // CHUNKS
    block = vocab // BLOCKS

    y = lax.axis_index('tp2')
    t = lax.axis_index('tp')
    core = lax.rem(t, CORES)
    x = lax.div(t, CORES)
    me = y * n1 + t
    f = x + core * (y - x)
    s = y + core * (x - y)
    mine = core * half + f * n2 + s

    def dev(a, b):
        return {'tp2': b + core * (a - b), 'tp': CORES * (a + core * (b - a)) + core}

    partner = {'tp2': y, 'tp': CORES * x + (1 - core)}

    def slab(a, b):
        return core * half + a * n2 + b

    def other(k):
        i = lax.rem(me + k, group)
        return {'tp2': lax.div(i, n1), 'tp': lax.rem(i, n1)}

    def remote(src, dst, ssem, rsem, to):
        return pltpu.make_async_remote_copy(src_ref=src, dst_ref=dst, send_sem=ssem, recv_sem=rsem,
                                            device_id=to, device_id_type=MESH)

    h0 = vocab - 3 * ff - rows
    g0, d_0 = h0 + rows, h0 + rows + 2 * ff
    first = [(hid.at[pl.ds(0, chunk)], wv.at[pl.ds(h0, chunk)]),
             (wg, wv.at[pl.ds(g0, ff)]), (wu, wv.at[pl.ds(g0 + ff, ff)]),
             (wd, wv.at[pl.ds(d_0, ff)]),
             (hid.at[pl.ds(chunk, rows - chunk)], wv.at[pl.ds(h0 + chunk, rows - chunk)])]
    head_rows = split(0, h0, 9)
    tail_rows = split(h0, vocab, 2)
    loads = [pltpu.make_async_copy(a, b, load_sem.at[i]) for i, (a, b) in enumerate(first)]
    loads += [pltpu.make_async_copy(wvt.at[pl.ds(a, n)], wv.at[pl.ds(a, n)], load_sem.at[len(first) + i])
              for i, (a, n) in enumerate(head_rows + tail_rows)]
    nf, nh = len(first), len(head_rows)
    for cp in loads[:nf]:
        cp.start()
    hcopy = [pltpu.make_async_copy(hid3.at[ch * group + mine], hs.at[ch], hs_sem.at[ch]) for ch in range(CHUNKS)]
    for cp in hcopy:
        cp.start()

    barrier = pltpu.get_barrier_semaphore()
    for k in range(1, group):
        pl.semaphore_signal(barrier, inc=1, device_id=other(k), device_id_type=MESH)

    def mlp(ch):
        gu = lax.dot_general(wv[pl.ds(g0, 2 * ff), :], wv[pl.ds(h0 + ch * chunk, chunk), :], NT,
                             preferred_element_type=F32)
        at = jax.nn.silu(gu[:ff]) * gu[ff:]
        act[...] = at.T.astype(BF16)
        step = 256
        for n in range(width // step):
            cols = pl.ds(n * step, step)
            part = jnp.dot(act[...], wv[pl.ds(d_0, ff), cols], preferred_element_type=F32)
            yp[ch, :, :, cols] = part.reshape(group, chunk // group, step).astype(BF16)

    def s0(ch):
        return remote(yp.at[ch, pl.ds((1 - core) * half, half)], d0.at[ch], s0_s.at[ch], s0_r.at[ch], partner)

    def s1(ch, d):
        to = lax.rem(f + d, n2)
        return remote(yp.at[ch, pl.ds(slab(to, 0), n2)], st1.at[ch, d - 1], s1_s.at[ch, d - 1],
                      s1_r.at[ch, d - 1], dev(to, s))

    def s2(ch, d):
        to = lax.rem(s + d, n2)
        return remote(yp.at[ch, slab(f, to)], st2.at[ch, d - 1], s2_s.at[ch, d - 1],
                      s2_r.at[ch, d - 1], dev(f, to))

    def add0(ch):
        s0(ch).wait_recv()

        def body(i, _):
            k = core * half + i
            yp[ch, k] = (yp[ch, k].astype(F32) + d0[ch, i].astype(F32)).astype(BF16)
            return 0
        lax.fori_loop(0, half, body, 0)

    def send1(ch):
        for d in (2, 1, 3):
            s1(ch, d).start()

    def add1(ch):
        for d in range(1, n2):
            s1(ch, d).wait_recv()

        def body(i, _):
            k = slab(f, i)
            acc = yp[ch, k].astype(F32)
            for d in range(n2 - 1):
                acc = acc + st1[ch, d, i].astype(F32)
            yp[ch, k] = acc.astype(BF16)
            return 0
        lax.fori_loop(0, n2, body, 0)

    def send2(ch):
        for d in (2, 1, 3):
            s2(ch, d).start()

    def norm(ch):
        hcopy[ch].wait()
        for d in range(1, n2):
            s2(ch, d).wait_recv()
        acc = yp[ch, mine].astype(F32)
        for d in range(n2 - 1):
            acc = acc + st2[ch, d].astype(F32)
        r = hs[ch].astype(F32) + acc.astype(BF16).astype(F32)
        inv = lax.rsqrt(jnp.mean(r * r, axis=-1, keepdims=True) + NORM_EPS)
        xf[ch, mine] = (gain[...] * r * inv).astype(BF16)

    def ga(ch, d):
        to = lax.rem(s + d, n2)
        ref = xf.at[ch, mine]
        return remote(ref, ref, ga_s.at[ch, d - 1], g_r.at[ch, mine], dev(f, to))

    def gb(ch, e, d):
        k = slab(f, lax.rem(s + n2 - e, n2))
        ref = xf.at[ch, k]
        return remote(ref, ref, gb_s.at[ch, e, d - 1], g_r.at[ch, k], dev(lax.rem(f + d, n2), s))

    def gc(ch, d, e):
        k = slab(lax.rem(f + n2 - d, n2), lax.rem(s + n2 - e, n2))
        ref = xf.at[ch, k]
        return remote(ref, ref, gc_s.at[ch, d, e], g_r.at[ch, k], partner)

    order = (0, 1, 3, 2)

    def gather_a(ch):
        for d in (2, 1, 3):
            ga(ch, d).start()
        for d in (2, 1, 3):
            gb(ch, 0, d).start()
        gc(ch, 0, 0).start()

    def got(ch, k):
        ref = xf.at[ch, k]
        remote(ref, ref, ga_s.at[ch, 0], g_r.at[ch, k], partner).wait_recv()

    def gather_b(ch):
        for e in order[1:]:
            got(ch, slab(f, lax.rem(s + n2 - e, n2)))
            for d in (2, 1, 3):
                gb(ch, e, d).start()
            gc(ch, 0, e).start()

    def gather_c(ch):
        for e in order:
            for d in order[1:]:
                got(ch, slab(lax.rem(f + n2 - d, n2), lax.rem(s + n2 - e, n2)))
                gc(ch, d, e).start()

    def gather_end(ch):
        for k in range(half):
            got(ch, (1 - core) * half + k)

        def body(j, _):
            v = xf[ch, pl.ds(2 * j, 2)].astype(F32).reshape(2 * (chunk // group), width)
            xm[ch, pl.ds(pl.multiple_of(j * 16, 16), 16), :] = v.astype(BF16)
            return 0
        lax.fori_loop(0, group // 2, body, 0)

    def head(ch, lo, hi, carry):
        cs = pl.ds(ch * chunk, chunk)
        inv_t = 1.0 / temp[0:1, cs]
        ids = tid[0:1, cs] - me * vocab

        def body(b, carry):
            m, sm, q, tg = carry
            rs = pl.ds(pl.multiple_of(b * block, 16), block)
            l = lax.dot_general(wv[rs, :], xm[ch], NT, preferred_element_type=F32) * inv_t
            lg[rs, cs] = l
            l3 = l.reshape(block // 8, 8, chunk)
            mn = jnp.maximum(m, jnp.max(l3, axis=0))
            a = jnp.exp(m - mn)
            e = jnp.exp(l3 - mn[None])
            row = (lax.broadcasted_iota(jnp.int32, l3.shape, 0) * 8
                   + lax.broadcasted_iota(jnp.int32, l3.shape, 1))
            hit = row == (ids - b * block)[None]
            return (mn, sm * a + jnp.sum(e, axis=0), q * a + jnp.sum(e * l3, axis=0),
                    tg + jnp.sum(jnp.where(hit, l3, 0.0), axis=0))
        return lax.fori_loop(lo, hi, body, carry)

    def start_carry():
        z = jnp.zeros((8, chunk), F32)
        return jnp.full((8, chunk), -3.4e38, F32), z, z, z

    def stat(ch, k):
        return remote(so.at[ch], sr.at[ch, me], so_s.at[ch, k - 1], so_r.at[ch, me], other(k))

    def stats_send(ch, carry):
        m8, s8, q8, t8 = carry
        m = jnp.max(m8, axis=0, keepdims=True)
        w = jnp.exp(m8 - m)
        so[ch, 0:1] = m
        so[ch, 1:2] = jnp.sum(s8 * w, axis=0, keepdims=True)
        so[ch, 2:3] = jnp.sum(q8 * w, axis=0, keepdims=True)
        so[ch, 3:4] = jnp.sum(t8, axis=0, keepdims=True)
        sr[ch, me] = so[ch]
        for k in range(1, group):
            stat(ch, k).start()

    def stats_end(ch):
        for k in range(1, group):
            i = lax.rem(me + k, group)
            remote(so.at[ch], sr.at[ch, i], so_s.at[ch, 0], so_r.at[ch, i], partner).wait_recv()
        m = sr[ch, :, 0, :]
        top = jnp.max(m, axis=0, keepdims=True)
        w = jnp.exp(m - top)
        total = jnp.sum(sr[ch, :, 1, :] * w, axis=0, keepdims=True)
        moment = jnp.sum(sr[ch, :, 2, :] * w, axis=0, keepdims=True)
        target = jnp.sum(sr[ch, :, 3, :], axis=0, keepdims=True)
        log_norm = top + jnp.log(total)
        cs = pl.ds(ch * chunk, chunk)
        stats[0:1, cs] = log_norm
        stats[1:2, cs] = log_norm - moment / total
        stats[2:3, cs] = target - log_norm

    for cp in loads[:nf - 1]:
        cp.wait()
    for cp in loads[nf:nf + nh]:
        cp.start()
    mlp(0)
    pl.semaphore_wait(barrier, group - 1)
    s0(0).start()
    loads[nf - 1].wait()
    mlp(1)
    s0(1).start()
    for cp in loads[nf + nh:]:
        cp.start()
    add0(0)
    send1(0)
    add0(1)
    add1(0)
    send2(0)
    send1(1)
    norm(0)
    gather_a(0)
    gather_b(0)
    gather_c(0)
    gather_end(0)
    add1(1)
    send2(1)
    for cp in loads[nf:]:
        cp.wait()
    carry = head(0, 0, 3, start_carry())
    norm(1)
    gather_a(1)
    carry = head(0, 3, 6, carry)
    gather_b(1)
    carry = head(0, 6, 9, carry)
    gather_c(1)
    carry = head(0, 9, BLOCKS, carry)
    stats_send(0, carry)
    gather_end(1)
    carry = head(1, 0, BLOCKS, start_carry())
    stats_send(1, carry)
    stats_end(0)
    stats_end(1)
    for ch in range(CHUNKS):
        s0(ch).wait_send()
        for d in range(1, n2):
            s1(ch, d).wait_send()
            s2(ch, d).wait_send()
            ga(ch, d).wait_send()
            for e in range(n2):
                gb(ch, e, d).wait_send()
        for d in range(n2):
            for e in range(n2):
                gc(ch, d, e).wait_send()
        for k in range(1, group):
            stat(ch, k).wait_send()


def final_kernel(lg, stats, out, buf, sem):
    vocab = lg.shape[0]
    step = buf.shape[1]
    steps, slots = vocab // step, buf.shape[0]

    def copy(i):
        return pltpu.make_async_copy(buf.at[i % slots], out.at[pl.ds(i * step, step)], sem.at[i % slots])

    for i in range(steps):
        if i >= slots:
            copy(i - slots).wait()
        buf[i % slots] = (lg[pl.ds(i * step, step), :] - stats[0:1, :]).astype(BF16)
        copy(i).start()
    for i in range(max(0, steps - slots), steps):
        copy(i).wait()


def solution(mesh):
    model_axes = ('tp2', 'tp')
    n2, n1 = mesh.shape['tp2'], mesh.shape['tp']
    group, nx = n2 * n1, n1 // CORES
    assert nx == n2

    def local_step(hidden, w_gate, w_up, w_down, norm_gain, w_vocab, temperature, target_ids):
        rows, width = hidden.shape
        ff, vocab = w_gate.shape[1], w_vocab.shape[1]
        chunk = rows // CHUNKS
        sl = chunk // group
        half = group // CORES
        hbm, vmem = pl.BlockSpec(memory_space=pl.ANY), pl.BlockSpec(memory_space=pltpu.VMEM)
        dma = pltpu.SemaphoreType.DMA
        c = CHUNKS
        lg, stats = pl.pallas_call(
            lambda *refs: main_kernel(n2, n1, *refs),
            out_shape=(pltpu.VMEM((vocab, rows), F32), pltpu.VMEM((3, rows), F32)),
            in_specs=[hbm] * 5 + [vmem, hbm, vmem, vmem],
            out_specs=(vmem, vmem),
            scratch_shapes=[
                pltpu.VMEM((vocab, width), BF16),
                pltpu.VMEM((c, group, sl, width), BF16),
                pltpu.VMEM((c, half, sl, width), BF16),
                pltpu.VMEM((c, n2 - 1, n2, sl, width), BF16),
                pltpu.VMEM((c, n2 - 1, sl, width), BF16),
                pltpu.VMEM((c, group, sl, width), BF16),
                pltpu.VMEM((c, chunk, width), BF16),
                pltpu.VMEM((c, sl, width), BF16),
                pltpu.VMEM((chunk, ff), BF16),
                pltpu.VMEM((c, 4, chunk), F32),
                pltpu.VMEM((c, group, 4, chunk), F32),
                dma((24,)), dma((c,)), dma((c,)), dma((c,)),
                dma((c, n2 - 1)), dma((c, n2 - 1)), dma((c, n2 - 1)), dma((c, n2 - 1)),
                dma((c, n2 - 1)), dma((c, n2, n2 - 1)), dma((c, n2, n2)), dma((c, group)),
                dma((c, group - 1)), dma((c, group)),
            ],
            name='mlp_head',
            cost_estimate=pl.CostEstimate(flops=2 * rows * width * (vocab + 3 * ff),
                                          bytes_accessed=2 * width * vocab, transcendentals=rows * vocab),
            compiler_params=pltpu.CompilerParams(collective_id=0, has_side_effects=True,
                                                 vmem_limit_bytes=47 * 1024 * 1024),
        )(hidden, hidden.reshape(rows // sl, sl, width), w_gate.T, w_up.T, w_down, norm_gain[None, :],
          w_vocab.T, temperature[None, :], target_ids[None, :])
        out = pl.pallas_call(
            final_kernel,
            out_shape=jax.ShapeDtypeStruct((vocab, rows), BF16),
            in_specs=[vmem, vmem],
            out_specs=hbm,
            scratch_shapes=[pltpu.VMEM((4, vocab // 20, rows), BF16), dma((4,))],
            name='logprobs',
            compiler_params=pltpu.CompilerParams(vmem_limit_bytes=16 * 1024 * 1024),
        )(lg, stats)
        return stats[0], stats[1], stats[2], out.T

    return jax.shard_map(
        local_step, mesh=mesh,
        in_specs=(P('dp', None), P(None, model_axes), P(None, model_axes), P(model_axes, None),
                  P(None), P(None, model_axes), P('dp'), P('dp')),
        out_specs=(P('dp'), P('dp'), P('dp'), P('dp', model_axes)),
        check_vma=False)
```

time: 264 us -> 80.8 us (0.31)
  waiting for transfers between devices: 102 us -> 0 us
  blocking collectives: 89.2 us -> 0 us
  Pallas kernels: 0 us -> 78 us
  matrix products: 35.8 us -> 0 us
  other arithmetic: 22 us -> 0 us
  between operations: 14.2 us -> 0.65 us
    psum x1 -> x0, waiting for transfers between devices: 102 us -> none  [local_step(): mlp_out = lax.psum(part_out, model_axes)]
    pallas_call x0 -> x2, Pallas kernels: none -> 78 us  [the longest x1 73.6 us: local_step(): pl.pallas_call(lambda *refs: main_kernel(n2, n1, *refs), out_shape=(pltpu...]
    pmax x1 -> x0, blocking collectives: 45.6 us -> none  [local_step(): global_max = lax.pmax(local_max, model_axes)]
    psum x1 -> x0, blocking collectives: 43.6 us -> none  [local_step(): totals = lax.psum(row_stats, model_axes)]
    dot_general x3 -> x0, matrix products: 35.8 us -> none  [the longest x1 27.4 us: local_step(): jnp.dot(normed, w_vocab, preferred_element_type=jnp.float32)]
    reduce_sum x2 -> x0, other arithmetic: 11.9 us -> none  [the longest x1 8.54 us: local_step(): local_sum = jnp.sum(shifted, axis=-1)]
    convert_element_type x1 -> x0, other arithmetic: 8.88 us -> none  [local_step(): logprobs = (logits - log_norm[:, None]).astype(jnp.bfloat16)]
  transfers between devices with their start and end apart: 1 -> 0, of which waited for: 1 -> 0; matrix products, arithmetic and copies ran while one was open for 0% -> 0% of each run, Pallas kernels for 0% -> 0%
where the time goes in v1:
time: 80.8 us; the launch traced here: 80.6 us
  Pallas kernels  78 us (97%)
  local copies, waits for them, and re-layouts  1.91 us (2%)
    pallas_call x1, Pallas kernels, local_step(): pl.pallas_call(lambda *refs: main_kernel(n2, n1, *refs), out_shape=(pltpu...  73.6 us
    pallas_call x1, Pallas kernels, local_step(): pl.pallas_call(final_kernel, out_shape=jax.ShapeDtypeStruct((vocab, rows)...  4.42 us

profile of v1, /device:TPU:97, one launch (start us, length us, event | category | flops | bytes accessed | tf_op | source)
XLA Modules:
  0.0 80.6 jit_solution(13238969320036403097)
XLA Ops:
  0.6 1.3 %broadcast_in_dim.9.refs_5_ = f32[1,2304]{1,0:T(1,128)} reshape(f32[2304]{0:T(1024)} %param.12) | data formatting | bytes 18432 | tf_op jit(solution)/shard_map/broadcast_in_dim | solution.py:369
  1.9 73.6 %mlp_head.1 = (f32[8000,512]{1,0:T(8,128)S(1)}, f32[3,512]{1,0:T(4,128)S(1)}) custom-call(bf16[512,2304]{1,0:T(8,128)(2,1)} %refs_0_.1, bf16[64,8,2304]{2,1,0:T(8,128)(2,1)} %bitcast.15, bf16[288,2304]{1,0:T(8,128)(2,1)} %bitcast.16, bf16[288,2304]{1,0:T(8,128)(2,1)} %bitcast.17, bf16[288,2304]{1,0:T(8,128)(2,1)} %refs_4_.1, ...), custom_call_target="tpu_custom_call" | custom-call | flops 20912799744 | bytes 36864000 | tf_op jit(solution)/shard_map/mlp_head/pallas_call | solution.py:342
  75.6 4.4 %logprobs.1 = bf16[8000,512]{1,0:T(8,128)(2,1)} custom-call(f32[8000,512]{1,0:T(8,128)S(1)} %get-tuple-element.7.lg, f32[3,512]{1,0:T(4,128)S(1)} %get-tuple-element.6.stats), custom_call_target="tpu_custom_call" | custom-call | tf_op jit(solution)/shard_map/logprobs/pallas_call | solution.py:371
  80.0 0.6 fusion

commit v2 on v0

v2 whole, which is shorter than its diff:
```python
import functools

import jax
import jax.numpy as jnp
from jax import lax
from jax.experimental import pallas as pl
from jax.experimental.pallas import tpu as pltpu
from jax.sharding import PartitionSpec as P

NORM_EPS = 1e-6
CORES = 2
HALVES = 2
BLOCKS = 20
UNROLL = 2
UNIT = 32
MESH = pl.DeviceIdType.MESH
NT = (((1,), (1,)), ((), ()))
F32, BF16 = jnp.float32, jnp.bfloat16


def split(start, stop, pieces):
    step = -(-(stop - start) // pieces)
    step = -(-step // 16) * 16
    return [(i, min(step, stop - i)) for i in range(start, stop, step)]


def main_kernel(n2, n1, hid, hid3, wg, wu, wd, gain, wvt, temp, tid, lg, stats,
                wv, yp, d0, fw, nb, st2, xf, hs, act, gain_v, temp_v, tid_v, so, pair_st, chip_st, sr, done,
                load_sem, hs_sem, small_sem, s0_s, s0_r, fw_s, fw_r, nb_s, nb_r, s2_s, s2_r,
                ga_s, gb_s, gf_s, gc_s, g_r, sw_s, sw_r, so_s, so_r):
    group = n1 * n2
    half = group // CORES
    rows, width = hid.shape
    ff = wg.shape[0]
    vocab = wvt.shape[0]
    chunk = rows // HALVES
    block = vocab // BLOCKS

    y = lax.axis_index('tp2')
    t = lax.axis_index('tp')
    core = lax.rem(t, CORES)
    x = lax.div(t, CORES)
    me = y * n1 + t
    f = y + core * (x - y)
    s = x + core * (y - x)
    mine = core * half + f * n2 + s

    def dev(a, b):
        return {'tp2': a + core * (b - a), 'tp': CORES * (b + core * (a - b)) + core}

    partner = {'tp2': y, 'tp': CORES * x + (1 - core)}

    def slab(a, b):
        return core * half + a * n2 + b

    def remote(src, dst, ssem, rsem, to):
        return pltpu.make_async_remote_copy(src_ref=src, dst_ref=dst, send_sem=ssem, recv_sem=rsem,
                                            device_id=to, device_id_type=MESH)

    right, left, far = (lax.rem(f + i, n2) for i in (1, n2 - 1, 2))
    peers = [dev(right, s), dev(left, s), partner] + [dev(f, lax.rem(s + d, n2)) for d in range(1, n2)]
    barrier = pltpu.get_barrier_semaphore()
    for p in peers:
        pl.semaphore_signal(barrier, inc=1, device_id=p, device_id_type=MESH)

    h0 = vocab - 3 * ff - rows
    g0, d_0 = h0 + rows, h0 + rows + 2 * ff
    theirs = pl.multiple_of((1 - core) * chunk, chunk)
    own = pl.multiple_of(core * chunk, chunk)
    first = [(hid.at[pl.ds(theirs, chunk)], wv.at[pl.ds(h0 + theirs, chunk)]),
             (wg, wv.at[pl.ds(g0, ff)]), (wu, wv.at[pl.ds(g0 + ff, ff)]),
             (wd, wv.at[pl.ds(d_0, ff)]),
             (hid.at[pl.ds(own, chunk)], wv.at[pl.ds(h0 + own, chunk)])]
    head_rows = split(0, h0, 9)
    tail_rows = split(h0, vocab, 2)
    loads = [pltpu.make_async_copy(a, b, load_sem.at[i]) for i, (a, b) in enumerate(first)]
    loads += [pltpu.make_async_copy(wvt.at[pl.ds(a, n)], wv.at[pl.ds(a, n)], load_sem.at[len(first) + i])
              for i, (a, n) in enumerate(head_rows + tail_rows)]
    nf, nh = len(first), len(head_rows)
    for cp in loads[:nf]:
        cp.start()
    hcopy = [pltpu.make_async_copy(hid3.at[mine], hs, hs_sem)]
    small = [pltpu.make_async_copy(a, b, small_sem.at[i])
             for i, (a, b) in enumerate(((gain, gain_v), (temp, temp_v), (tid, tid_v)))]
    for cp in hcopy + small:
        cp.start()

    def gate_up(ch):
        gu = lax.dot_general(wv[pl.ds(g0, 2 * ff), :], wv[pl.ds(pl.multiple_of(h0 + ch * chunk, 16), chunk), :], NT,
                             preferred_element_type=F32)
        at = jax.nn.silu(gu[:ff]) * gu[ff:]
        act[...] = at.T.astype(BF16)

    def down(ch):
        step = 256
        for n in range(width // step):
            cols = pl.ds(n * step, step)
            part = jnp.dot(act[...], wv[pl.ds(d_0, ff), cols], preferred_element_type=F32)
            yp[pl.ds(ch * half, half), :, cols] = part.reshape(half, rows // group, step).astype(BF16)

    def s0():
        return remote(yp.at[pl.ds((1 - core) * half, half)], d0, s0_s, s0_r, partner)

    LATE = ((2, 1), (3, 0))

    def at_s(d):
        return lax.rem(s + d, n2)

    def send_fw(i, j):
        return remote(yp.at[slab(far, at_s(LATE[i][j]))], fw.at[i, j], fw_s.at[i, j],
                      fw_r.at[i, j], dev((right, left)[i], s))

    def send_nb(i, d):
        to = (right, left)[i]
        return remote(yp.at[slab(to, at_s(d))], nb.at[i, d], nb_s.at[i, d],
                      nb_r.at[i, d], dev(to, s))

    def s2(d):
        to = lax.rem(s + d, n2)
        return remote(yp.at[slab(f, to)], st2.at[d - 1], s2_s.at[d - 1],
                      s2_r.at[d - 1], dev(f, to))

    def add0():
        s0().wait_recv()

        def body(i, _):
            k = core * half + i
            yp[k] = (yp[k].astype(F32) + d0[i].astype(F32)).astype(BF16)
            return 0
        lax.fori_loop(0, half, body, 0)

    def send1():
        for j in (0, 1):
            for i in (0, 1):
                send_fw(i, j).start()
        for j in (0, 1):
            for i in (0, 1):
                send_nb(i, LATE[1 - i][j]).start()

    def pass1():
        for j in (0, 1):
            for i in (0, 1):
                d = LATE[i][j]
                send_fw(i, j).wait_recv()
                k = slab((right, left)[i], at_s(d))
                yp[k] = (yp[k].astype(F32) + fw[i, j].astype(F32)).astype(BF16)
                send_nb(i, d).start()

    def add1():
        for d in (2, 3, 1, 0):
            for i in (0, 1):
                send_nb(i, d).wait_recv()
            k = slab(f, at_s(d))
            yp[k] = (yp[k].astype(F32) + nb[0, d].astype(F32) + nb[1, d].astype(F32)).astype(BF16)
            if d:
                s2(d).start()

    def norm():
        for d in range(1, n2):
            s2(d).wait_recv()
        acc = yp[mine].astype(F32)
        for d in range(n2 - 1):
            acc = acc + st2[d].astype(F32)
        r = hs[...].astype(F32) + acc.astype(BF16).astype(F32)
        inv = lax.rsqrt(jnp.mean(r * r, axis=-1, keepdims=True) + NORM_EPS)
        xf[mine] = (gain_v[...].reshape(1, width) * r * inv).astype(BF16)

    def ga(d):
        ref = xf.at[mine]
        return remote(ref, ref, ga_s.at[d - 1], g_r.at[mine], dev(f, at_s(d)))

    def back(a, e):
        return slab(a, at_s(n2 - e))

    def gb(i, e):
        k = back(f, e)
        ref = xf.at[k]
        return remote(ref, ref, gb_s.at[i, e], g_r.at[k], dev((right, left)[i], s))

    PASS = ((0, 1), (3, 2))

    def gf(i, j):
        k = back((left, right)[i], PASS[i][j])
        ref = xf.at[k]
        return remote(ref, ref, gf_s.at[i, j], g_r.at[k], dev((right, left)[i], s))

    def gc(d, e):
        k = back(lax.rem(f + d, n2), e)
        ref = xf.at[k]
        return remote(ref, ref, gc_s.at[d, e], g_r.at[k], partner)

    def got(k):
        ref = xf.at[k]
        remote(ref, ref, ga_s.at[0], g_r.at[k], partner).wait_recv()

    def out_own(e):
        if e:
            got(back(f, e))
        for i in (0, 1):
            gb(i, e).start()
        gc(0, e).start()

    def from_side(e):
        for i in ((0, 1) if e in PASS[0] else (1, 0)):
            got(back((left, right)[i], e))
            if e in PASS[i]:
                gf(i, PASS[i].index(e)).start()
            gc((n2 - 1, 1)[i], e).start()

    def from_far(e):
        got(back(far, e))
        gc(2, e).start()

    def gather(part):
        if part == 0:
            for d in (2, 1, 3):
                ga(d).start()
            out_own(0)
        elif part == 1:
            out_own(1)
            out_own(3)
        elif part == 2:
            from_side(0)
            out_own(2)
        elif part == 3:
            from_side(1)
            from_side(3)
        elif part == 4:
            from_far(0)
            from_side(2)
        else:
            for e in (1, 3, 2):
                from_far(e)

    def gather_end():
        for k in range(half):
            got((1 - core) * half + k)

    def head():
        inv_t = 1.0 / temp_v[...]
        lanes = lax.broadcasted_iota(jnp.int32, (8, rows), 0)
        ids = tid_v[...] - me * vocab - lanes

        def products(i):
            for u in range(UNROLL):
                rs = pl.ds(pl.multiple_of((i * UNROLL + u) * block, 16), block)
                l = lax.dot_general(wv[rs, :], xf[...].reshape(rows, width), NT, preferred_element_type=F32)
                lg[rs, :] = l * inv_t

        def update(i, carry):
            m, total, moment, target = carry
            for u in range(UNROLL):
                base = (i * UNROLL + u) * block
                here = ids - base
                for g in range(0, block, UNIT):
                    n = min(UNIT, block - g)
                    l = lg[pl.ds(pl.multiple_of(base + g, 8), n), :]
                    parts = [l[j:j + 8] for j in range(0, n, 8)]
                    tops = parts
                    while len(tops) > 1:
                        tops = [jnp.maximum(*tops[j:j + 2]) if j + 1 < len(tops) else tops[j]
                                for j in range(0, len(tops), 2)]
                    top = jnp.maximum(m, tops[0])
                    scale = jnp.exp(m - top)
                    total, moment, m = total * scale, moment * scale, top
                    for j, p in enumerate(parts):
                        e = jnp.exp(p - top)
                        total, moment = total + e, moment + e * p
                        target = jnp.where(here == g + 8 * j, p, target)
            return m, total, moment, target

        def body(i, carry):
            carry = update(i - 1, carry)
            products(i)
            return carry

        z = jnp.zeros((8, rows), F32)
        products(0)
        steps = BLOCKS // UNROLL
        carry = lax.fori_loop(1, steps, body, (jnp.full((8, rows), -3.4e38, F32), z, z, z))
        return update(steps - 1, carry)

    chips = group // CORES
    chip = y * (n1 // CORES) + x

    def swap(src, dst, k):
        return remote(src, dst, sw_s.at[k], sw_r.at[k], partner)

    def stat(k):
        i = lax.rem(chip + k, chips)
        to = {'tp2': lax.div(i, n1 // CORES), 'tp': CORES * lax.rem(i, n1 // CORES) + core}
        return remote(chip_st, sr.at[chip], so_s.at[k - 1], so_r.at[chip], to)

    def statistics(carry):
        m8, s8, q8, t8 = carry
        m = jnp.max(m8, axis=0, keepdims=True)
        w = jnp.exp(m8 - m)
        rows4 = [m, jnp.sum(s8 * w, axis=0, keepdims=True), jnp.sum(q8 * w, axis=0, keepdims=True),
                 jnp.sum(t8, axis=0, keepdims=True)]
        for j in range(4):
            for h in range(HALVES):
                so[h, j:j + 1] = rows4[j][:, h * chunk:(h + 1) * chunk]
        first = swap(so.at[1 - core], pair_st, 0)
        first.start()
        first.wait_recv()
        a, b = so[core], pair_st[...]
        m = jnp.maximum(a[0:1], b[0:1])
        wa, wb = jnp.exp(a[0:1] - m), jnp.exp(b[0:1] - m)
        chip_st[0:1] = m
        chip_st[1:3] = a[1:3] * wa + b[1:3] * wb
        chip_st[3:4] = a[3:4] + b[3:4]
        for k in range(1, chips):
            stat(k).start()
        sr[chip] = chip_st[...]
        for k in range(1, chips):
            i = lax.rem(chip + k, chips)
            remote(chip_st, sr.at[i], so_s.at[0], so_r.at[i], partner).wait_recv()
        m = sr[:, 0, :]
        top = jnp.max(m, axis=0, keepdims=True)
        w = jnp.exp(m - top)
        total = jnp.sum(sr[:, 1, :] * w, axis=0, keepdims=True)
        moment = jnp.sum(sr[:, 2, :] * w, axis=0, keepdims=True)
        log_norm = top + jnp.log(total)
        done[core, 0:1] = log_norm
        done[core, 1:2] = log_norm - moment / total
        done[core, 2:3] = jnp.sum(sr[:, 3, :], axis=0, keepdims=True) - log_norm
        second = swap(done.at[core], done.at[core], 1)
        second.start()
        swap(done.at[1 - core], done.at[1 - core], 1).wait_recv()
        for h in range(HALVES):
            stats[:, h * chunk:(h + 1) * chunk] = done[h, 0:3]
        first.wait_send()
        second.wait_send()
        for k in range(1, chips):
            stat(k).wait_send()

    for cp in loads[:nf - 1]:
        cp.wait()
    for cp in loads[nf:nf + nh]:
        cp.start()
    gate_up(1 - core)
    down(1 - core)
    pl.semaphore_wait(barrier, len(peers))
    s0().start()
    loads[nf - 1].wait()
    gate_up(core)
    down(core)
    for cp in loads[nf + nh:]:
        cp.start()
    add0()
    send1()
    pass1()
    for cp in hcopy + small:
        cp.wait()
    add1()
    norm()
    for part in range(6):
        gather(part)
    gather_end()
    for cp in loads[nf:]:
        cp.wait()
    carry = head()
    statistics(carry)
    s0().wait_send()
    for i in (0, 1):
        for j in (0, 1):
            send_fw(i, j).wait_send()
            gf(i, j).wait_send()
        for d in range(n2):
            send_nb(i, d).wait_send()
            gb(i, d).wait_send()
    for d in range(1, n2):
        s2(d).wait_send()
        ga(d).wait_send()
    for d in range(n2):
        for e in range(n2):
            gc(d, e).wait_send()


def final_kernel(lg, stats, out, *rest):
    outs, rows, (buf, sem, row_sem) = rest[:3], rest[3:6], rest[6:]
    vocab = lg.shape[0]
    step = buf.shape[1]
    steps, slots = vocab // step, buf.shape[0]

    def copy(i):
        return pltpu.make_async_copy(buf.at[i % slots], out.at[pl.ds(i * step, step)], sem.at[i % slots])

    for i in range(steps):
        if i >= slots:
            copy(i - slots).wait()
        buf[i % slots] = (lg[pl.ds(i * step, step), :] - stats[0:1, :]).astype(BF16)
        copy(i).start()
        if i == 0:
            small = [pltpu.make_async_copy(rows[j], outs[j], row_sem.at[j]) for j in range(3)]
            for j in range(3):
                rows[j][...] = stats[j, :]
            for cp in small:
                cp.start()
    for cp in small:
        cp.wait()
    for i in range(max(0, steps - slots), steps):
        copy(i).wait()


def solution(mesh):
    model_axes = ('tp2', 'tp')
    n2, n1 = mesh.shape['tp2'], mesh.shape['tp']
    group, nx = n2 * n1, n1 // CORES
    assert nx == n2

    def local_step(hidden, w_gate, w_up, w_down, norm_gain, w_vocab, temperature, target_ids):
        rows, width = hidden.shape
        ff, vocab = w_gate.shape[1], w_vocab.shape[1]
        sl = rows // group
        half = group // CORES
        hbm, vmem = pl.BlockSpec(memory_space=pl.ANY), pl.BlockSpec(memory_space=pltpu.VMEM)
        dma = pltpu.SemaphoreType.DMA
        lg, stats = pl.pallas_call(
            lambda *refs: main_kernel(n2, n1, *refs),
            out_shape=(pltpu.VMEM((vocab, rows), F32), pltpu.VMEM((3, rows), F32)),
            in_specs=[hbm] * 9,
            out_specs=(vmem, vmem),
            scratch_shapes=[
                pltpu.VMEM((vocab, width), BF16),
                pltpu.VMEM((group, sl, width), BF16),
                pltpu.VMEM((half, sl, width), BF16),
                pltpu.VMEM((2, 2, sl, width), BF16),
                pltpu.VMEM((2, n2, sl, width), BF16),
                pltpu.VMEM((n2 - 1, sl, width), BF16),
                pltpu.VMEM((group, sl, width), BF16),
                pltpu.VMEM((sl, width), BF16),
                pltpu.VMEM((rows // HALVES, ff), BF16),
                pltpu.VMEM((width,), F32),
                pltpu.VMEM((1, rows), F32),
                pltpu.VMEM((1, rows), jnp.int32),
                pltpu.VMEM((HALVES, 4, rows // HALVES), F32),
                pltpu.VMEM((4, rows // HALVES), F32),
                pltpu.VMEM((4, rows // HALVES), F32),
                pltpu.VMEM((half, 4, rows // HALVES), F32),
                pltpu.VMEM((HALVES, 4, rows // HALVES), F32),
                dma((24,)), dma, dma((3,)), dma, dma,
                dma((2, 2)), dma((2, 2)), dma((2, n2)), dma((2, n2)), dma((n2 - 1,)), dma((n2 - 1,)),
                dma((n2 - 1,)), dma((2, n2)), dma((2, 2)), dma((n2, n2)), dma((group,)),
                dma((2,)), dma((2,)), dma((half - 1,)), dma((half,)),
            ],
            name='mlp_head',
            cost_estimate=pl.CostEstimate(flops=2 * rows * width * (vocab + 3 * ff),
                                          bytes_accessed=2 * width * vocab, transcendentals=rows * vocab),
            compiler_params=pltpu.CompilerParams(collective_id=0, has_side_effects=True,
                                                 vmem_limit_bytes=47 * 1024 * 1024),
        )(hidden, hidden.reshape(group, sl, width), w_gate.T, w_up.T, w_down, norm_gain,
          w_vocab.T, temperature[None, :], target_ids[None, :])
        row = jax.ShapeDtypeStruct((rows,), F32)
        out, *small = pl.pallas_call(
            final_kernel,
            out_shape=(jax.ShapeDtypeStruct((vocab, rows), BF16), row, row, row),
            in_specs=[vmem, vmem],
            out_specs=(hbm,) * 4,
            scratch_shapes=[pltpu.VMEM((rows,), F32)] * 3 + [pltpu.VMEM((4, vocab // 10, rows), BF16), dma((4,)), dma((3,))],
            name='logprobs',
            compiler_params=pltpu.CompilerParams(vmem_limit_bytes=16 * 1024 * 1024),
        )(lg, stats)
        return *small, out.T

    return jax.shard_map(
        local_step, mesh=mesh,
        in_specs=(P('dp', None), P(None, model_axes), P(None, model_axes), P(model_axes, None),
                  P(None), P(None, model_axes), P('dp'), P('dp')),
        out_specs=(P('dp'), P('dp'), P('dp'), P('dp', model_axes)),
        check_vma=False)
```

time: 264 us -> 77.1 us (0.29)
  waiting for transfers between devices: 102 us -> 0 us
  blocking collectives: 89.2 us -> 0 us
  Pallas kernels: 0 us -> 76.4 us
  matrix products: 35.8 us -> 0 us
  other arithmetic: 22 us -> 0 us
  between operations: 14.2 us -> 0.64 us
    psum x1 -> x0, waiting for transfers between devices: 102 us -> none  [local_step(): mlp_out = lax.psum(part_out, model_axes)]
    pallas_call x0 -> x2, Pallas kernels: none -> 76.4 us  [the longest x1 73 us: local_step(): pl.pallas_call(lambda *refs: main_kernel(n2, n1, *refs), out_shape=(pltpu...]
    pmax x1 -> x0, blocking collectives: 45.6 us -> none  [local_step(): global_max = lax.pmax(local_max, model_axes)]
    psum x1 -> x0, blocking collectives: 43.6 us -> none  [local_step(): totals = lax.psum(row_stats, model_axes)]
    dot_general x3 -> x0, matrix products: 35.8 us -> none  [the longest x1 27.4 us: local_step(): jnp.dot(normed, w_vocab, preferred_element_type=jnp.float32)]
    reduce_sum x2 -> x0, other arithmetic: 11.9 us -> none  [the longest x1 8.54 us: local_step(): local_sum = jnp.sum(shifted, axis=-1)]
    convert_element_type x1 -> x0, other arithmetic: 8.88 us -> none  [local_step(): logprobs = (logits - log_norm[:, None]).astype(jnp.bfloat16)]
  transfers between devices with their start and end apart: 1 -> 0, of which waited for: 1 -> 0; matrix products, arithmetic and copies ran while one was open for 0% -> 0% of each run, Pallas kernels for 0% -> 0%
where the time goes in v2:
time: 77.1 us
  Pallas kernels  76.4 us (99%)
    pallas_call x1, Pallas kernels, local_step(): pl.pallas_call(lambda *refs: main_kernel(n2, n1, *refs), out_shape=(pltpu...  73 us
    pallas_call x1, Pallas kernels, local_step(): pl.pallas_call(final_kernel, out_shape=(jax.ShapeDtypeStruct((vocab, rows...  3.41 us

profile of v2, /device:TPU:97, one launch (start us, length us, event | category | flops | bytes accessed | tf_op | source)
XLA Modules:
  0.0 77.1 jit_solution(13885558187862975416)
XLA Ops:
  0.6 73.0 %mlp_head.1 = (f32[8000,512]{1,0:T(8,128)S(1)}, f32[3,512]{1,0:T(4,128)S(1)}) custom-call(bf16[512,2304]{1,0:T(8,128)(2,1)} %refs_0_.1, bf16[32,16,2304]{2,1,0:T(8,128)(2,1)} %bitcast.9, bf16[288,2304]{1,0:T(8,128)(2,1)} %bitcast.10, bf16[288,2304]{1,0:T(8,128)(2,1)} %bitcast.11, bf16[288,2304]{1,0:T(8,128)(2,1)} %refs_4_.1, f32[2304]{0:T(1024)} %refs_5_.1, ...), custom_call_target="tpu_custom_call" | custom-call | flops 20912799744 | bytes 36864000 | tf_op jit(solution)/shard_map/mlp_head/pallas_call | solution.py:419
  73.6 3.4 %logprobs.1 = (bf16[8000,512]{1,0:T(8,128)(2,1)}, f32[512]{0:T(512)}, f32[512]{0:T(512)}, f32[512]{0:T(512)}) custom-call(f32[8000,512]{1,0:T(8,128)S(1)} %get-tuple-element.10.lg, f32[3,512]{1,0:T(4,128)S(1)} %get-tuple-element.11.stats), custom_call_target="tpu_custom_call" | custom-call | tf_op jit(solution)/shard_map/logprobs/pallas_call | solution.py:455

commit v3 on v2

--- a/solution.py
+++ b/solution.py
@@ -10,6 +10,7 @@
 NORM_EPS = 1e-6
 CORES = 2
 HALVES = 2
+CHUNKS = 2
 BLOCKS = 20
 UNROLL = 2
 UNIT = 32
@@ -25,7 +26,7 @@
 
 
 def main_kernel(n2, n1, hid, hid3, wg, wu, wd, gain, wvt, temp, tid, lg, stats,
-                wv, yp, d0, fw, nb, st2, xf, hs, act, gain_v, temp_v, tid_v, so, pair_st, chip_st, sr, done,
+                wv, yp, d0, fw, nb, st2, xf, xm, hs, act, gain_v, temp_v, tid_v, so, pair_st, chip_st, sr, done,
                 load_sem, hs_sem, small_sem, s0_s, s0_r, fw_s, fw_r, nb_s, nb_r, s2_s, s2_r,
                 ga_s, gb_s, gf_s, gc_s, g_r, sw_s, sw_r, so_s, so_r):
     group = n1 * n2
@@ -33,7 +34,7 @@
     rows, width = hid.shape
     ff = wg.shape[0]
     vocab = wvt.shape[0]
-    chunk = rows // HALVES
+    chunk = rows // CHUNKS
     block = vocab // BLOCKS
 
     y = lax.axis_index('tp2')
@@ -65,12 +66,15 @@
 
     h0 = vocab - 3 * ff - rows
     g0, d_0 = h0 + rows, h0 + rows + 2 * ff
-    theirs = pl.multiple_of((1 - core) * chunk, chunk)
-    own = pl.multiple_of(core * chunk, chunk)
-    first = [(hid.at[pl.ds(theirs, chunk)], wv.at[pl.ds(h0 + theirs, chunk)]),
-             (wg, wv.at[pl.ds(g0, ff)]), (wu, wv.at[pl.ds(g0 + ff, ff)]),
-             (wd, wv.at[pl.ds(d_0, ff)]),
-             (hid.at[pl.ds(own, chunk)], wv.at[pl.ds(h0 + own, chunk)])]
+    quarter = chunk // CORES
+    need = [1 - core, core]
+
+    def rows_of(j):
+        return [(hid.at[pl.ds(pl.multiple_of(ch * chunk + need[j] * quarter, quarter), quarter)],
+                 wv.at[pl.ds(h0 + j * chunk + ch * quarter, quarter)]) for ch in range(CHUNKS)]
+
+    first = [(wg, wv.at[pl.ds(g0, ff)]), (wu, wv.at[pl.ds(g0 + ff, ff)])] + rows_of(0) + rows_of(1)
+    first += [(wd, wv.at[pl.ds(d_0, ff)])]
     head_rows = split(0, h0, 9)
     tail_rows = split(h0, vocab, 2)
     loads = [pltpu.make_async_copy(a, b, load_sem.at[i]) for i, (a, b) in enumerate(first)]
@@ -79,162 +83,170 @@
     nf, nh = len(first), len(head_rows)
     for cp in loads[:nf]:
         cp.start()
-    hcopy = [pltpu.make_async_copy(hid3.at[mine], hs, hs_sem)]
+    hcopy = [pltpu.make_async_copy(hid3.at[ch * group + mine], hs.at[ch], hs_sem.at[ch]) for ch in range(CHUNKS)]
     small = [pltpu.make_async_copy(a, b, small_sem.at[i])
              for i, (a, b) in enumerate(((gain, gain_v), (temp, temp_v), (tid, tid_v)))]
     for cp in hcopy + small:
         cp.start()
 
-    def gate_up(ch):
-        gu = lax.dot_general(wv[pl.ds(g0, 2 * ff), :], wv[pl.ds(pl.multiple_of(h0 + ch * chunk, 16), chunk), :], NT,
-                             preferred_element_type=F32)
+    def gate_up():
+        gu = lax.dot_general(wv[pl.ds(g0, 2 * ff), :], wv[pl.ds(h0, rows), :], NT, preferred_element_type=F32)
         at = jax.nn.silu(gu[:ff]) * gu[ff:]
         act[...] = at.T.astype(BF16)
 
-    def down(ch):
+    def down(j):
         step = 256
         for n in range(width // step):
             cols = pl.ds(n * step, step)
-            part = jnp.dot(act[...], wv[pl.ds(d_0, ff), cols], preferred_element_type=F32)
-            yp[pl.ds(ch * half, half), :, cols] = part.reshape(half, rows // group, step).astype(BF16)
-
-    def s0():
-        return remote(yp.at[pl.ds((1 - core) * half, half)], d0, s0_s, s0_r, partner)
+            part = jnp.dot(act[pl.ds(j * chunk, chunk), :], wv[pl.ds(d_0, ff), cols], preferred_element_type=F32)
+            yp[:, pl.ds(need[j] * half, half), :, cols] = part.reshape(
+                CHUNKS, half, chunk // group, step).astype(BF16)
+
+    def s0(ch):
+        return remote(yp.at[ch, pl.ds((1 - core) * half, half)], d0.at[ch], s0_s.at[ch], s0_r.at[ch], partner)
 
     LATE = ((2, 1), (3, 0))
 
     def at_s(d):
         return lax.rem(s + d, n2)
 
-    def send_fw(i, j):
-        return remote(yp.at[slab(far, at_s(LATE[i][j]))], fw.at[i, j], fw_s.at[i, j],
-                      fw_r.at[i, j], dev((right, left)[i], s))
-
-    def send_nb(i, d):
+    def send_fw(ch, i, j):
+        return remote(yp.at[ch, slab(far, at_s(LATE[i][j]))], fw.at[ch, i, j], fw_s.at[ch, i, j],
+                      fw_r.at[ch, i, j], dev((right, left)[i], s))
+
+    def send_nb(ch, i, d):
         to = (right, left)[i]
-        return remote(yp.at[slab(to, at_s(d))], nb.at[i, d], nb_s.at[i, d],
-                      nb_r.at[i, d], dev(to, s))
-
-    def s2(d):
+        return remote(yp.at[ch, slab(to, at_s(d))], nb.at[ch, i, d], nb_s.at[ch, i, d],
+                      nb_r.at[ch, i, d], dev(to, s))
+
+    def s2(ch, d):
         to = lax.rem(s + d, n2)
-        return remote(yp.at[slab(f, to)], st2.at[d - 1], s2_s.at[d - 1],
-                      s2_r.at[d - 1], dev(f, to))
-
-    def add0():
-        s0().wait_recv()
+        return remote(yp.at[ch, slab(f, to)], st2.at[ch, d - 1], s2_s.at[ch, d - 1],
+                      s2_r.at[ch, d - 1], dev(f, to))
+
+    def add0(ch):
+        s0(ch).wait_recv()
 
         def body(i, _):
             k = core * half + i
-            yp[k] = (yp[k].astype(F32) + d0[i].astype(F32)).astype(BF16)
+            yp[ch, k] = (yp[ch, k].astype(F32) + d0[ch, i].astype(F32)).astype(BF16)
             return 0
         lax.fori_loop(0, half, body, 0)
 
-    def send1():
+    def send1(ch):
         for j in (0, 1):
             for i in (0, 1):
-                send_fw(i, j).start()
+                send_fw(ch, i, j).start()
+
+    def send1b(ch):
         for j in (0, 1):
             for i in (0, 1):
-                send_nb(i, LATE[1 - i][j]).start()
-
-    def pass1():
+                send_nb(ch, i, LATE[1 - i][j]).start()
+
+    def pass1(ch):
         for j in (0, 1):
             for i in (0, 1):
                 d = LATE[i][j]
-                send_fw(i, j).wait_recv()
+                send_fw(ch, i, j).wait_recv()
                 k = slab((right, left)[i], at_s(d))
-                yp[k] = (yp[k].astype(F32) + fw[i, j].astype(F32)).astype(BF16)
-                send_nb(i, d).start()
-
-    def add1():
+                yp[ch, k] = (yp[ch, k].astype(F32) + fw[ch, i, j].astype(F32)).astype(BF16)
+                send_nb(ch, i, d).start()
+
+    def add1(ch):
         for d in (2, 3, 1, 0):
             for i in (0, 1):
-                send_nb(i, d).wait_recv()
+                send_nb(ch, i, d).wait_recv()
             k = slab(f, at_s(d))
-            yp[k] = (yp[k].astype(F32) + nb[0, d].astype(F32) + nb[1, d].astype(F32)).astype(BF16)
+            yp[ch, k] = (yp[ch, k].astype(F32) + nb[ch, 0, d].astype(F32) + nb[ch, 1, d].astype(F32)).astype(BF16)
             if d:
-                s2(d).start()
-
-    def norm():
+                s2(ch, d).start()
+
+    def norm(ch):
         for d in range(1, n2):
-            s2(d).wait_recv()
-        acc = yp[mine].astype(F32)
+            s2(ch, d).wait_recv()
+        acc = yp[ch, mine].astype(F32)
         for d in range(n2 - 1):
-            acc = acc + st2[d].astype(F32)
-        r = hs[...].astype(F32) + acc.astype(BF16).astype(F32)
+            acc = acc + st2[ch, d].astype(F32)
+        r = hs[ch].astype(F32) + acc.astype(BF16).astype(F32)
         inv = lax.rsqrt(jnp.mean(r * r, axis=-1, keepdims=True) + NORM_EPS)
-        xf[mine] = (gain_v[...].reshape(1, width) * r * inv).astype(BF16)
-
-    def ga(d):
-        ref = xf.at[mine]
-        return remote(ref, ref, ga_s.at[d - 1], g_r.at[mine], dev(f, at_s(d)))
+        xf[ch, mine] = (gain_v[...].reshape(1, width) * r * inv).astype(BF16)
+
+    def ga(ch, d):
+        ref = xf.at[ch, mine]
+        return remote(ref, ref, ga_s.at[ch, d - 1], g_r.at[ch, mine], dev(f, at_s(d)))
 
     def back(a, e):
         return slab(a, at_s(n2 - e))
 
-    def gb(i, e):
+    def gb(ch, i, e):
         k = back(f, e)
-        ref = xf.at[k]
-        return remote(ref, ref, gb_s.at[i, e], g_r.at[k], dev((right, left)[i], s))
+        ref = xf.at[ch, k]
+        return remote(ref, ref, gb_s.at[ch, i, e], g_r.at[ch, k], dev((right, left)[i], s))
 
     PASS = ((0, 1), (3, 2))
 
-    def gf(i, j):
+    def gf(ch, i, j):
         k = back((left, right)[i], PASS[i][j])
-        ref = xf.at[k]
-        return remote(ref, ref, gf_s.at[i, j], g_r.at[k], dev((right, left)[i], s))
-
-    def gc(d, e):
+        ref = xf.at[ch, k]
+        return remote(ref, ref, gf_s.at[ch, i, j], g_r.at[ch, k], dev((right, left)[i], s))
+
+    def gc(ch, d, e):
         k = back(lax.rem(f + d, n2), e)
-        ref = xf.at[k]
-        return remote(ref, ref, gc_s.at[d, e], g_r.at[k], partner)
-
-    def got(k):
-        ref = xf.at[k]
-        remote(ref, ref, ga_s.at[0], g_r.at[k], partner).wait_recv()
-
-    def out_own(e):
+        ref = xf.at[ch, k]
+        return remote(ref, ref, gc_s.at[ch, d, e], g_r.at[ch, k], partner)
+
+    def got(ch, k):
+        ref = xf.at[ch, k]
+        remote(ref, ref, ga_s.at[ch, 0], g_r.at[ch, k], partner).wait_recv()
+
+    def out_own(ch, e):
         if e:
-            got(back(f, e))
+            got(ch, back(f, e))
         for i in (0, 1):
-            gb(i, e).start()
-        gc(0, e).start()
-
-    def from_side(e):
+            gb(ch, i, e).start()
+        gc(ch, 0, e).start()
+
+    def from_side(ch, e):
         for i in ((0, 1) if e in PASS[0] else (1, 0)):
-            got(back((left, right)[i], e))
+            got(ch, back((left, right)[i], e))
             if e in PASS[i]:
-                gf(i, PASS[i].index(e)).start()
-            gc((n2 - 1, 1)[i], e).start()
-
-    def from_far(e):
-        got(back(far, e))
-        gc(2, e).start()
-
-    def gather(part):
+                gf(ch, i, PASS[i].index(e)).start()
+            gc(ch, (n2 - 1, 1)[i], e).start()
+
+    def from_far(ch, e):
+        got(ch, back(far, e))
+        gc(ch, 2, e).start()
+
+    def gather(ch, part):
         if part == 0:
             for d in (2, 1, 3):
-                ga(d).start()
-            out_own(0)
+                ga(ch, d).start()
+            out_own(ch, 0)
         elif part == 1:
-            out_own(1)
-            out_own(3)
+            out_own(ch, 1)
+            out_own(ch, 3)
         elif part == 2:
-            from_side(0)
-            out_own(2)
+            from_side(ch, 0)
+            out_own(ch, 2)
         elif part == 3:
-            from_side(1)
-            from_side(3)
+            from_side(ch, 1)
+            from_side(ch, 3)
         elif part == 4:
-            from_far(0)
-            from_side(2)
+            from_far(ch, 0)
+            from_side(ch, 2)
         else:
             for e in (1, 3, 2):
-                from_far(e)
-
-    def gather_end():
+                from_far(ch, e)
+
+    def gather_end(ch):
         for k in range(half):
-            got((1 - core) * half + k)
+            got(ch, (1 - core) * half + k)
+
+        def body(j, _):
+            v = xf[ch, pl.ds(2 * j, 2)].astype(F32).reshape(2 * (chunk // group), width)
+            xm[pl.ds(pl.multiple_of(ch * chunk + j * 16, 16), 16), :] = v.astype(BF16)
+            return 0
+        lax.fori_loop(0, group // 2, body, 0)
 
     def head():
         inv_t = 1.0 / temp_v[...]
@@ -244,7 +256,7 @@
         def products(i):
             for u in range(UNROLL):
                 rs = pl.ds(pl.multiple_of((i * UNROLL + u) * block, 16), block)
-                l = lax.dot_general(wv[rs, :], xf[...].reshape(rows, width), NT, preferred_element_type=F32)
+                l = lax.dot_general(wv[rs, :], xm[...], NT, preferred_element_type=F32)
                 lg[rs, :] = l * inv_t
 
         def update(i, carry):
@@ -336,45 +348,64 @@
 
     for cp in loads[:nf - 1]:
         cp.wait()
+    gate_up()
+    loads[nf - 1].wait()
     for cp in loads[nf:nf + nh]:
         cp.start()
-    gate_up(1 - core)
-    down(1 - core)
+    down(0)
     pl.semaphore_wait(barrier, len(peers))
-    s0().start()
-    loads[nf - 1].wait()
-    gate_up(core)
-    down(core)
+    s0(0).start()
+    s0(1).start()
+    down(1)
     for cp in loads[nf + nh:]:
         cp.start()
-    add0()
-    send1()
-    pass1()
+    add0(0)
+    send1(0)
+    add0(1)
+    send1(1)
+    send1b(0)
+    send1b(1)
+    pass1(0)
+    pass1(1)
     for cp in hcopy + small:
         cp.wait()
-    add1()
-    norm()
-    for part in range(6):
-        gather(part)
-    gather_end()
+    add1(0)
+    add1(1)
+    norm(0)
+    gather(0, 0)
+    norm(1)
+    gather(1, 0)
+    gather(0, 1)
+    gather(1, 1)
+    gather(0, 2)
+    gather(1, 2)
+    gather(0, 3)
+    gather(1, 3)
+    gather(0, 4)
+    gather(1, 4)
+    gather(0, 5)
+    gather(1, 5)
+    gather_end(0)
+    gather_end(1)
     for cp in loads[nf:]:
         cp.wait()
     carry = head()
     statistics(carry)
-    s0().wait_send()
-    for i in (0, 1):
-        for j in (0, 1):
-            send_fw(i, j).wait_send()
-            gf(i, j).wait_send()
+    for ch in range(CHUNKS):
+        s0(ch).wait_send()
+        for i in (0, 1):
+            for j in (0, 1):
+                send_fw(ch, i, j).wait_send()
+                gf(ch, i, j).wait_send()
+            for d in range(n2):
+                send_nb(ch, i, d).wait_send()
+                gb(ch, i, d).wait_send()
+        for d in range(1, n2):
+            s2(ch, d).wait_send()
+            ga(ch, d).wait_send()
         for d in range(n2):
-            send_nb(i, d).wait_send()
-            gb(i, d).wait_send()
-    for d in range(1, n2):
-        s2(d).wait_send()
-        ga(d).wait_send()
-    for d in range(n2):
-        for e in range(n2):
-            gc(d, e).wait_send()
+            for e in range(n2):
+                gc(ch, d, e).wait_send()
 
 
 def final_kernel(lg, stats, out, *rest):
@@ -412,10 +443,12 @@
     def local_step(hidden, w_gate, w_up, w_down, norm_gain, w_vocab, temperature, target_ids):
         rows, width = hidden.shape
         ff, vocab = w_gate.shape[1], w_vocab.shape[1]
-        sl = rows // group
+        chunk = rows // CHUNKS
+        sl = chunk // group
         half = group // CORES
         hbm, vmem = pl.BlockSpec(memory_space=pl.ANY), pl.BlockSpec(memory_space=pltpu.VMEM)
         dma = pltpu.SemaphoreType.DMA
+        c = CHUNKS
         lg, stats = pl.pallas_call(
             lambda *refs: main_kernel(n2, n1, *refs),
             out_shape=(pltpu.VMEM((vocab, rows), F32), pltpu.VMEM((3, rows), F32)),
@@ -423,14 +456,15 @@
             out_specs=(vmem, vmem),
             scratch_shapes=[
                 pltpu.VMEM((vocab, width), BF16),
-                pltpu.VMEM((group, sl, width), BF16),
-                pltpu.VMEM((half, sl, width), BF16),
-                pltpu.VMEM((2, 2, sl, width), BF16),
-                pltpu.VMEM((2, n2, sl, width), BF16),
-                pltpu.VMEM((n2 - 1, sl, width), BF16),
-                pltpu.VMEM((group, sl, width), BF16),
-                pltpu.VMEM((sl, width), BF16),
-                pltpu.VMEM((rows // HALVES, ff), BF16),
+                pltpu.VMEM((c, group, sl, width), BF16),
+                pltpu.VMEM((c, half, sl, width), BF16),
+                pltpu.VMEM((c, 2, 2, sl, width), BF16),
+                pltpu.VMEM((c, 2, n2, sl, width), BF16),
+                pltpu.VMEM((c, n2 - 1, sl, width), BF16),
+                pltpu.VMEM((c, group, sl, width), BF16),
+                pltpu.VMEM((rows, width), BF16),
+                pltpu.VMEM((c, sl, width), BF16),
+                pltpu.VMEM((rows, ff), BF16),
                 pltpu.VMEM((width,), F32),
                 pltpu.VMEM((1, rows), F32),
                 pltpu.VMEM((1, rows), jnp.int32),
@@ -439,9 +473,9 @@
                 pltpu.VMEM((4, rows // HALVES), F32),
                 pltpu.VMEM((half, 4, rows // HALVES), F32),
                 pltpu.VMEM((HALVES, 4, rows // HALVES), F32),
-                dma((24,)), dma, dma((3,)), dma, dma,
-                dma((2, 2)), dma((2, 2)), dma((2, n2)), dma((2, n2)), dma((n2 - 1,)), dma((n2 - 1,)),
-                dma((n2 - 1,)), dma((2, n2)), dma((2, 2)), dma((n2, n2)), dma((group,)),
+                dma((24,)), dma((c,)), dma((3,)), dma((c,)), dma((c,)),
+                dma((c, 2, 2)), dma((c, 2, 2)), dma((c, 2, n2)), dma((c, 2, n2)), dma((c, n2 - 1)), dma((c, n2 - 1)),
+                dma((c, n2 - 1)), dma((c, 2, n2)), dma((c, 2, 2)), dma((c, n2, n2)), dma((c, group)),
                 dma((2,)), dma((2,)), dma((half - 1,)), dma((half,)),
             ],
             name='mlp_head',
@@ -449,7 +483,7 @@
                                           bytes_accessed=2 * width * vocab, transcendentals=rows * vocab),
             compiler_params=pltpu.CompilerParams(collective_id=0, has_side_effects=True,
                                                  vmem_limit_bytes=47 * 1024 * 1024),
-        )(hidden, hidden.reshape(group, sl, width), w_gate.T, w_up.T, w_down, norm_gain,
+        )(hidden, hidden.reshape(rows // sl, sl, width), w_gate.T, w_up.T, w_down, norm_gain,
           w_vocab.T, temperature[None, :], target_ids[None, :])
         row = jax.ShapeDtypeStruct((rows,), F32)
         out, *small = pl.pallas_call(

time: 77.1 us -> 73.6 us (0.955)
  Pallas kernels: 76.4 us -> 72.8 us
    pallas_call x1, Pallas kernels: 73 us -> 69.4 us  [local_step(): pl.pallas_call(lambda *refs: main_kernel(n2, n1, *refs), out_shape=(pltpu...]
where the time goes in v3:
time: 73.6 us; the launch traced here: 73.5 us
  Pallas kernels  72.8 us (99%)
    pallas_call x1, Pallas kernels, local_step(): pl.pallas_call(lambda *refs: main_kernel(n2, n1, *refs), out_shape=(pltpu...  69.4 us
    pallas_call x1, Pallas kernels, local_step(): pl.pallas_call(final_kernel, out_shape=(jax.ShapeDtypeStruct((vocab, rows...  3.41 us

profile of v3, /device:TPU:97, one launch (start us, length us, event | category | flops | bytes accessed | tf_op | source)
XLA Modules:
  0.0 73.5 jit_solution(2222795288067779132)
XLA Ops:
  0.6 69.4 %mlp_head.1 = (f32[8000,512]{1,0:T(8,128)S(1)}, f32[3,512]{1,0:T(4,128)S(1)}) custom-call(bf16[512,2304]{1,0:T(8,128)(2,1)} %refs_0_.1, bf16[64,8,2304]{2,1,0:T(8,128)(2,1)} %bitcast.9, bf16[288,2304]{1,0:T(8,128)(2,1)} %bitcast.10, bf16[288,2304]{1,0:T(8,128)(2,1)} %bitcast.11, bf16[288,2304]{1,0:T(8,128)(2,1)} %refs_4_.1, f32[2304]{0:T(1024)} %refs_5_.1, ...), custom_call_target="tpu_custom_call" | custom-call | flops 20912799744 | bytes 36864000 | tf_op jit(solution)/shard_map/mlp_head/pallas_call | solution.py:452
  70.1 3.4 %logprobs.1 = (bf16[8000,512]{1,0:T(8,128)(2,1)}, f32[512]{0:T(512)}, f32[512]{0:T(512)}, f32[512]{0:T(512)}) custom-call(f32[8000,512]{1,0:T(8,128)S(1)} %get-tuple-element.10.lg, f32[3,512]{1,0:T(4,128)S(1)} %get-tuple-element.11.stats), custom_call_target="tpu_custom_call" | custom-call | tf_op jit(solution)/shard_map/logprobs/pallas_call | solution.py:489

commit v4 on v3

--- a/solution.py
+++ b/solution.py
@@ -28,7 +28,7 @@
 def main_kernel(n2, n1, hid, hid3, wg, wu, wd, gain, wvt, temp, tid, lg, stats,
                 wv, yp, d0, fw, nb, st2, xf, xm, hs, act, gain_v, temp_v, tid_v, so, pair_st, chip_st, sr, done,
                 load_sem, hs_sem, small_sem, s0_s, s0_r, fw_s, fw_r, nb_s, nb_r, s2_s, s2_r,
-                ga_s, gb_s, gf_s, gc_s, g_r, sw_s, sw_r, so_s, so_r):
+                ga_s, gb_s, gf_s, gd_s, gc_s, g_r, sw_s, sw_r, so_s, so_r):
     group = n1 * n2
     half = group // CORES
     rows, width = hid.shape
@@ -183,7 +183,11 @@
         ref = xf.at[ch, k]
         return remote(ref, ref, gb_s.at[ch, i, e], g_r.at[ch, k], dev((right, left)[i], s))
 
-    PASS = ((0, 1), (3, 2))
+    PASS = ((0, 1), (3,))
+
+    def gd(ch):
+        ref = xf.at[ch, mine]
+        return remote(ref, ref, gd_s.at[ch], g_r.at[ch, mine], dev(far, at_s(2)))
 
     def gf(ch, i, j):
         k = back((left, right)[i], PASS[i][j])
@@ -222,6 +226,7 @@
             for d in (2, 1, 3):
                 ga(ch, d).start()
             out_own(ch, 0)
+            gd(ch).start()
         elif part == 1:
             out_own(ch, 1)
             out_own(ch, 3)
@@ -233,9 +238,10 @@
             from_side(ch, 3)
         elif part == 4:
             from_far(ch, 0)
+            from_far(ch, 2)
             from_side(ch, 2)
         else:
-            for e in (1, 3, 2):
+            for e in (1, 3):
                 from_far(ch, e)
 
     def gather_end(ch):
@@ -396,10 +402,12 @@
         for i in (0, 1):
             for j in (0, 1):
                 send_fw(ch, i, j).wait_send()
+            for j in range(len(PASS[i])):
                 gf(ch, i, j).wait_send()
             for d in range(n2):
                 send_nb(ch, i, d).wait_send()
                 gb(ch, i, d).wait_send()
+        gd(ch).wait_send()
         for d in range(1, n2):
             s2(ch, d).wait_send()
             ga(ch, d).wait_send()
@@ -475,7 +483,7 @@
                 pltpu.VMEM((HALVES, 4, rows // HALVES), F32),
                 dma((24,)), dma((c,)), dma((3,)), dma((c,)), dma((c,)),
                 dma((c, 2, 2)), dma((c, 2, 2)), dma((c, 2, n2)), dma((c, 2, n2)), dma((c, n2 - 1)), dma((c, n2 - 1)),
-                dma((c, n2 - 1)), dma((c, 2, n2)), dma((c, 2, 2)), dma((c, n2, n2)), dma((c, group)),
+                dma((c, n2 - 1)), dma((c, 2, n2)), dma((c, 2, 2)), dma((c,)), dma((c, n2, n2)), dma((c, group)),
                 dma((2,)), dma((2,)), dma((half - 1,)), dma((half,)),
             ],
             name='mlp_head',

time: 73.6 us -> 72.7 us (0.988)
  Pallas kernels: 72.8 us -> 72 us
    pallas_call x1, Pallas kernels: 69.4 us -> 68.5 us  [local_step(): pl.pallas_call(lambda *refs: main_kernel(n2, n1, *refs), out_shape=(pltpu...]
where the time goes in v4:
time: 72.7 us; the launch traced here: 72.6 us
  Pallas kernels  72 us (99%)
    pallas_call x1, Pallas kernels, local_step(): pl.pallas_call(lambda *refs: main_kernel(n2, n1, *refs), out_shape=(pltpu...  68.5 us
    pallas_call x1, Pallas kernels, local_step(): pl.pallas_call(final_kernel, out_shape=(jax.ShapeDtypeStruct((vocab, rows...  3.41 us

profile of v4, /device:TPU:97, one launch (start us, length us, event | category | flops | bytes accessed | tf_op | source)
XLA Modules:
  0.0 72.6 jit_solution(18228878684475616467)
XLA Ops:
  0.6 68.5 %mlp_head.1 = (f32[8000,512]{1,0:T(8,128)S(1)}, f32[3,512]{1,0:T(4,128)S(1)}) custom-call(bf16[512,2304]{1,0:T(8,128)(2,1)} %refs_0_.1, bf16[64,8,2304]{2,1,0:T(8,128)(2,1)} %bitcast.9, bf16[288,2304]{1,0:T(8,128)(2,1)} %bitcast.10, bf16[288,2304]{1,0:T(8,128)(2,1)} %bitcast.11, bf16[288,2304]{1,0:T(8,128)(2,1)} %refs_4_.1, f32[2304]{0:T(1024)} %refs_5_.1, ...), custom_call_target="tpu_custom_call" | custom-call | flops 20912799744 | bytes 36864000 | tf_op jit(solution)/shard_map/mlp_head/pallas_call | solution.py:460
  69.2 3.4 %logprobs.1 = (bf16[8000,512]{1,0:T(8,128)(2,1)}, f32[512]{0:T(512)}, f32[512]{0:T(512)}, f32[512]{0:T(512)}) custom-call(f32[8000,512]{1,0:T(8,128)S(1)} %get-tuple-element.10.lg, f32[3,512]{1,0:T(4,128)S(1)} %get-tuple-element.11.stats), custom_call_target="tpu_custom_call" | custom-call | tf_op jit(solution)/shard_map/logprobs/pallas_call | solution.py:497

commit v5 on v4

--- a/solution.py
+++ b/solution.py
@@ -10,6 +10,7 @@
 NORM_EPS = 1e-6
 CORES = 2
 HALVES = 2
+PARTS = 3
 CHUNKS = 2
 BLOCKS = 20
 UNROLL = 2
@@ -28,7 +29,7 @@
 def main_kernel(n2, n1, hid, hid3, wg, wu, wd, gain, wvt, temp, tid, lg, stats,
                 wv, yp, d0, fw, nb, st2, xf, xm, hs, act, gain_v, temp_v, tid_v, so, pair_st, chip_st, sr, done,
                 load_sem, hs_sem, small_sem, s0_s, s0_r, fw_s, fw_r, nb_s, nb_r, s2_s, s2_r,
-                ga_s, gb_s, gf_s, gd_s, gc_s, g_r, sw_s, sw_r, so_s, so_r):
+                ga_s, gb_s, gf_s, gd_s, gs_s, gc_s, g_r, sw_s, sw_r, so_s, so_r):
     group = n1 * n2
     half = group // CORES
     rows, width = hid.shape
@@ -60,10 +61,6 @@
 
     right, left, far = (lax.rem(f + i, n2) for i in (1, n2 - 1, 2))
     peers = [dev(right, s), dev(left, s), partner] + [dev(f, lax.rem(s + d, n2)) for d in range(1, n2)]
-    barrier = pltpu.get_barrier_semaphore()
-    for p in peers:
-        pl.semaphore_signal(barrier, inc=1, device_id=p, device_id_type=MESH)
-
     h0 = vocab - 3 * ff - rows
     g0, d_0 = h0 + rows, h0 + rows + 2 * ff
     quarter = chunk // CORES
@@ -83,6 +80,9 @@
     nf, nh = len(first), len(head_rows)
     for cp in loads[:nf]:
         cp.start()
+    barrier = pltpu.get_barrier_semaphore()
+    for p in peers:
+        pl.semaphore_signal(barrier, inc=1, device_id=p, device_id_type=MESH)
     hcopy = [pltpu.make_async_copy(hid3.at[ch * group + mine], hs.at[ch], hs_sem.at[ch]) for ch in range(CHUNKS)]
     small = [pltpu.make_async_copy(a, b, small_sem.at[i])
              for i, (a, b) in enumerate(((gain, gain_v), (temp, temp_v), (tid, tid_v)))]
@@ -94,16 +94,20 @@
         at = jax.nn.silu(gu[:ff]) * gu[ff:]
         act[...] = at.T.astype(BF16)
 
-    def down(j):
+    def down(j, after=None):
         step = 256
         for n in range(width // step):
             cols = pl.ds(n * step, step)
             part = jnp.dot(act[pl.ds(j * chunk, chunk), :], wv[pl.ds(d_0, ff), cols], preferred_element_type=F32)
             yp[:, pl.ds(need[j] * half, half), :, cols] = part.reshape(
                 CHUNKS, half, chunk // group, step).astype(BF16)
-
-    def s0(ch):
-        return remote(yp.at[ch, pl.ds((1 - core) * half, half)], d0.at[ch], s0_s.at[ch], s0_r.at[ch], partner)
+            if after is not None and (n + 1) % (width // step // PARTS) == 0:
+                after((n + 1) // (width // step // PARTS) - 1)
+
+    def s0(ch, part):
+        cols = pl.ds(part * (width // PARTS), width // PARTS)
+        return remote(yp.at[ch, pl.ds((1 - core) * half, half), :, cols], d0.at[ch, :, :, cols],
+                      s0_s.at[ch, part], s0_r.at[ch, part], partner)
 
     LATE = ((2, 1), (3, 0))
 
@@ -125,7 +129,8 @@
                       s2_r.at[ch, d - 1], dev(f, to))
 
     def add0(ch):
-        s0(ch).wait_recv()
+        for part in range(PARTS):
+            s0(ch, part).wait_recv()
 
         def body(i, _):
             k = core * half + i
@@ -183,14 +188,20 @@
         ref = xf.at[ch, k]
         return remote(ref, ref, gb_s.at[ch, i, e], g_r.at[ch, k], dev((right, left)[i], s))
 
-    PASS = ((0, 1), (3,))
+    PASS = (((0, 1), (3,)), ((0, 1), ()))
+    STRAIGHT = ((), (3,))
+
+    def gs(ch, e):
+        k = back(f, e)
+        ref = xf.at[ch, k]
+        return remote(ref, ref, gs_s.at[ch, e], g_r.at[ch, k], dev(far, s))
 
     def gd(ch):
         ref = xf.at[ch, mine]
         return remote(ref, ref, gd_s.at[ch], g_r.at[ch, mine], dev(far, at_s(2)))
 
     def gf(ch, i, j):
-        k = back((left, right)[i], PASS[i][j])
+        k = back((left, right)[i], PASS[ch][i][j])
         ref = xf.at[ch, k]
         return remote(ref, ref, gf_s.at[ch, i, j], g_r.at[ch, k], dev((right, left)[i], s))
 
@@ -208,13 +219,15 @@
             got(ch, back(f, e))
         for i in (0, 1):
             gb(ch, i, e).start()
+        if e in STRAIGHT[ch]:
+            gs(ch, e).start()
         gc(ch, 0, e).start()
 
     def from_side(ch, e):
-        for i in ((0, 1) if e in PASS[0] else (1, 0)):
+        for i in ((0, 1) if e < 2 else (1, 0)):
             got(ch, back((left, right)[i], e))
-            if e in PASS[i]:
-                gf(ch, i, PASS[i].index(e)).start()
+            if e in PASS[ch][i]:
+                gf(ch, i, PASS[ch][i].index(e)).start()
             gc(ch, (n2 - 1, 1)[i], e).start()
 
     def from_far(ch, e):
@@ -358,10 +371,10 @@
     loads[nf - 1].wait()
     for cp in loads[nf:nf + nh]:
         cp.start()
-    down(0)
     pl.semaphore_wait(barrier, len(peers))
-    s0(0).start()
-    s0(1).start()
+    down(0, lambda part: s0(0, part).start())
+    for part in range(PARTS):
+        s0(1, part).start()
     down(1)
     for cp in loads[nf + nh:]:
         cp.start()
@@ -398,16 +411,19 @@
     carry = head()
     statistics(carry)
     for ch in range(CHUNKS):
-        s0(ch).wait_send()
+        for part in range(PARTS):
+            s0(ch, part).wait_send()
         for i in (0, 1):
             for j in (0, 1):
                 send_fw(ch, i, j).wait_send()
-            for j in range(len(PASS[i])):
+            for j in range(len(PASS[ch][i])):
                 gf(ch, i, j).wait_send()
             for d in range(n2):
                 send_nb(ch, i, d).wait_send()
                 gb(ch, i, d).wait_send()
         gd(ch).wait_send()
+        for e in STRAIGHT[ch]:
+            gs(ch, e).wait_send()
         for d in range(1, n2):
             s2(ch, d).wait_send()
             ga(ch, d).wait_send()
@@ -419,16 +435,19 @@
 def final_kernel(lg, stats, out, *rest):
     outs, rows, (buf, sem, row_sem) = rest[:3], rest[3:6], rest[6:]
     vocab = lg.shape[0]
-    step = buf.shape[1]
-    steps, slots = vocab // step, buf.shape[0]
+    step, slots = buf.shape[1], buf.shape[0]
+    sizes = [step // 2] + [step] * (vocab // step - 1) + [step // 2]
+    starts = [sum(sizes[:i]) for i in range(len(sizes))]
+    steps = len(sizes)
 
     def copy(i):
-        return pltpu.make_async_copy(buf.at[i % slots], out.at[pl.ds(i * step, step)], sem.at[i % slots])
+        return pltpu.make_async_copy(buf.at[i % slots, pl.ds(0, sizes[i])], out.at[pl.ds(starts[i], sizes[i])],
+                                     sem.at[i % slots])
 
     for i in range(steps):
         if i >= slots:
             copy(i - slots).wait()
-        buf[i % slots] = (lg[pl.ds(i * step, step), :] - stats[0:1, :]).astype(BF16)
+        buf[i % slots, 0:sizes[i]] = (lg[pl.ds(starts[i], sizes[i]), :] - stats[0:1, :]).astype(BF16)
         copy(i).start()
         if i == 0:
             small = [pltpu.make_async_copy(rows[j], outs[j], row_sem.at[j]) for j in range(3)]
@@ -481,9 +500,9 @@
                 pltpu.VMEM((4, rows // HALVES), F32),
                 pltpu.VMEM((half, 4, rows // HALVES), F32),
                 pltpu.VMEM((HALVES, 4, rows // HALVES), F32),
-                dma((24,)), dma((c,)), dma((3,)), dma((c,)), dma((c,)),
+                dma((24,)), dma((c,)), dma((3,)), dma((c, PARTS)), dma((c, PARTS)),
                 dma((c, 2, 2)), dma((c, 2, 2)), dma((c, 2, n2)), dma((c, 2, n2)), dma((c, n2 - 1)), dma((c, n2 - 1)),
-                dma((c, n2 - 1)), dma((c, 2, n2)), dma((c, 2, 2)), dma((c,)), dma((c, n2, n2)), dma((c, group)),
+                dma((c, n2 - 1)), dma((c, 2, n2)), dma((c, 2, 2)), dma((c,)), dma((c, n2)), dma((c, n2, n2)), dma((c, group)),
                 dma((2,)), dma((2,)), dma((half - 1,)), dma((half,)),
             ],
             name='mlp_head',

time: 72.7 us -> 71.6 us (0.985)
  Pallas kernels: 72 us -> 70.9 us
    pallas_call x1, Pallas kernels: 68.5 us -> 67.5 us  [local_step(): pl.pallas_call(lambda *refs: main_kernel(n2, n1, *refs), out_shape=(pltpu...]
where the time goes in v5:
time: 71.6 us; the launch traced here: 71.5 us
  Pallas kernels  70.9 us (99%)
    pallas_call x1, Pallas kernels, local_step(): pl.pallas_call(lambda *refs: main_kernel(n2, n1, *refs), out_shape=(pltpu...  67.5 us
    pallas_call x1, Pallas kernels, local_step(): pl.pallas_call(final_kernel, out_shape=(jax.ShapeDtypeStruct((vocab, rows...  3.34 us

profile of v5, /device:TPU:97, one launch (start us, length us, event | category | flops | bytes accessed | tf_op | source)
XLA Modules:
  0.0 71.5 jit_solution(10888992407794671936)
XLA Ops:
  0.6 67.5 %mlp_head.1 = (f32[8000,512]{1,0:T(8,128)S(1)}, f32[3,512]{1,0:T(4,128)S(1)}) custom-call(bf16[512,2304]{1,0:T(8,128)(2,1)} %refs_0_.1, bf16[64,8,2304]{2,1,0:T(8,128)(2,1)} %bitcast.9, bf16[288,2304]{1,0:T(8,128)(2,1)} %bitcast.10, bf16[288,2304]{1,0:T(8,128)(2,1)} %bitcast.11, bf16[288,2304]{1,0:T(8,128)(2,1)} %refs_4_.1, f32[2304]{0:T(1024)} %refs_5_.1, ...), custom_call_target="tpu_custom_call" | custom-call | flops 20912799744 | bytes 36864000 | tf_op jit(solution)/shard_map/mlp_head/pallas_call | solution.py:479
  68.2 3.3 %logprobs.1 = (bf16[8000,512]{1,0:T(8,128)(2,1)}, f32[512]{0:T(512)}, f32[512]{0:T(512)}, f32[512]{0:T(512)}) custom-call(f32[8000,512]{1,0:T(8,128)S(1)} %get-tuple-element.10.lg, f32[3,512]{1,0:T(4,128)S(1)} %get-tuple-element.11.stats), custom_call_target="tpu_custom_call" | custom-call | tf_op jit(solution)/shard_map/logprobs/pallas_call | solution.py:516

commit v6 on v5

--- a/solution.py
+++ b/solution.py
@@ -27,7 +27,7 @@
 
 
 def main_kernel(n2, n1, hid, hid3, wg, wu, wd, gain, wvt, temp, tid, lg, stats,
-                wv, yp, d0, fw, nb, st2, xf, xm, hs, act, gain_v, temp_v, tid_v, so, pair_st, chip_st, sr, done,
+                wv, yp, d0, fw, nb, st2, xf, xm, hs, act, gain_v, temp_v, tid_v, so, sr, done,
                 load_sem, hs_sem, small_sem, s0_s, s0_r, fw_s, fw_r, nb_s, nb_r, s2_s, s2_r,
                 ga_s, gb_s, gf_s, gd_s, gs_s, gc_s, g_r, sw_s, sw_r, so_s, so_r):
     group = n1 * n2
@@ -251,10 +251,9 @@
             from_side(ch, 3)
         elif part == 4:
             from_far(ch, 0)
-            from_far(ch, 2)
             from_side(ch, 2)
         else:
-            for e in (1, 3):
+            for e in (1, 3, 2):
                 from_far(ch, e)
 
     def gather_end(ch):
@@ -312,15 +311,29 @@
         return update(steps - 1, carry)
 
     chips = group // CORES
-    chip = y * (n1 // CORES) + x
 
     def swap(src, dst, k):
         return remote(src, dst, sw_s.at[k], sw_r.at[k], partner)
 
-    def stat(k):
-        i = lax.rem(chip + k, chips)
-        to = {'tp2': lax.div(i, n1 // CORES), 'tp': CORES * lax.rem(i, n1 // CORES) + core}
-        return remote(chip_st, sr.at[chip], so_s.at[k - 1], so_r.at[chip], to)
+    nx = n1 // CORES
+    others = sorted(((a, b) for a in range(n2) for b in range(nx) if a or b),
+                    key=lambda o: -min(o[0], n2 - o[0]) - min(o[1], nx - o[1]))
+
+    def other_chip(k):
+        a, b = others[k - 1]
+        return lax.rem(y + a, n2), lax.rem(x + b, nx)
+
+    def stat(k, same):
+        a, b = other_chip(k) if k else (y, x)
+        to = core if same else 1 - core
+        return remote(so.at[to], sr.at[me], so_s.at[same, k], so_r.at[me], {'tp2': a, 'tp': CORES * b + to})
+
+    def stat_from(k, same):
+        a, b = other_chip(k) if k else (y, x)
+        i = a * n1 + CORES * b + (core if same else 1 - core)
+        return remote(so.at[0], sr.at[i], so_s.at[same, k], so_r.at[i], partner)
+
+    targets = [(k, same) for k in range(1, chips) for same in (0, 1)] + [(0, 0)]
 
     def statistics(carry):
         m8, s8, q8, t8 = carry
@@ -331,21 +344,11 @@
         for j in range(4):
             for h in range(HALVES):
                 so[h, j:j + 1] = rows4[j][:, h * chunk:(h + 1) * chunk]
-        first = swap(so.at[1 - core], pair_st, 0)
-        first.start()
-        first.wait_recv()
-        a, b = so[core], pair_st[...]
-        m = jnp.maximum(a[0:1], b[0:1])
-        wa, wb = jnp.exp(a[0:1] - m), jnp.exp(b[0:1] - m)
-        chip_st[0:1] = m
-        chip_st[1:3] = a[1:3] * wa + b[1:3] * wb
-        chip_st[3:4] = a[3:4] + b[3:4]
-        for k in range(1, chips):
-            stat(k).start()
-        sr[chip] = chip_st[...]
-        for k in range(1, chips):
-            i = lax.rem(chip + k, chips)
-            remote(chip_st, sr.at[i], so_s.at[0], so_r.at[i], partner).wait_recv()
+        for k, same in targets:
+            stat(k, same).start()
+        sr[me] = so[core]
+        for k, same in targets:
+            stat_from(k, same).wait_recv()
         m = sr[:, 0, :]
         top = jnp.max(m, axis=0, keepdims=True)
         w = jnp.exp(m - top)
@@ -355,15 +358,14 @@
         done[core, 0:1] = log_norm
         done[core, 1:2] = log_norm - moment / total
         done[core, 2:3] = jnp.sum(sr[:, 3, :], axis=0, keepdims=True) - log_norm
-        second = swap(done.at[core], done.at[core], 1)
+        second = swap(done.at[core], done.at[core], 0)
         second.start()
-        swap(done.at[1 - core], done.at[1 - core], 1).wait_recv()
+        swap(done.at[1 - core], done.at[1 - core], 0).wait_recv()
         for h in range(HALVES):
             stats[:, h * chunk:(h + 1) * chunk] = done[h, 0:3]
-        first.wait_send()
         second.wait_send()
-        for k in range(1, chips):
-            stat(k).wait_send()
+        for k, same in targets:
+            stat(k, same).wait_send()
 
     for cp in loads[:nf - 1]:
         cp.wait()
@@ -496,14 +498,12 @@
                 pltpu.VMEM((1, rows), F32),
                 pltpu.VMEM((1, rows), jnp.int32),
                 pltpu.VMEM((HALVES, 4, rows // HALVES), F32),
-                pltpu.VMEM((4, rows // HALVES), F32),
-                pltpu.VMEM((4, rows // HALVES), F32),
-                pltpu.VMEM((half, 4, rows // HALVES), F32),
+                pltpu.VMEM((group, 4, rows // HALVES), F32),
                 pltpu.VMEM((HALVES, 4, rows // HALVES), F32),
                 dma((24,)), dma((c,)), dma((3,)), dma((c, PARTS)), dma((c, PARTS)),
                 dma((c, 2, 2)), dma((c, 2, 2)), dma((c, 2, n2)), dma((c, 2, n2)), dma((c, n2 - 1)), dma((c, n2 - 1)),
                 dma((c, n2 - 1)), dma((c, 2, n2)), dma((c, 2, 2)), dma((c,)), dma((c, n2)), dma((c, n2, n2)), dma((c, group)),
-                dma((2,)), dma((2,)), dma((half - 1,)), dma((half,)),
+                dma((1,)), dma((1,)), dma((2, half)), dma((group,)),
             ],
             name='mlp_head',
             cost_estimate=pl.CostEstimate(flops=2 * rows * width * (vocab + 3 * ff),

time: 71.6 us -> 71.1 us (level)
  no operation moved by 1% of the time
where the time goes in v6:
time: 71.1 us; the launch traced here: 71 us
  Pallas kernels  70.4 us (99%)
    pallas_call x1, Pallas kernels, local_step(): pl.pallas_call(lambda *refs: main_kernel(n2, n1, *refs), out_shape=(pltpu...  67.1 us
    pallas_call x1, Pallas kernels, local_step(): pl.pallas_call(final_kernel, out_shape=(jax.ShapeDtypeStruct((vocab, rows...  3.34 us

profile of v6, /device:TPU:97, one launch (start us, length us, event | category | flops | bytes accessed | tf_op | source)
XLA Modules:
  0.0 71.0 jit_solution(17291594811666549836)
XLA Ops:
  0.6 67.1 %mlp_head.1 = (f32[8000,512]{1,0:T(8,128)S(1)}, f32[3,512]{1,0:T(4,128)S(1)}) custom-call(bf16[512,2304]{1,0:T(8,128)(2,1)} %refs_0_.1, bf16[64,8,2304]{2,1,0:T(8,128)(2,1)} %bitcast.9, bf16[288,2304]{1,0:T(8,128)(2,1)} %bitcast.10, bf16[288,2304]{1,0:T(8,128)(2,1)} %bitcast.11, bf16[288,2304]{1,0:T(8,128)(2,1)} %refs_4_.1, f32[2304]{0:T(1024)} %refs_5_.1, ...), custom_call_target="tpu_custom_call" | custom-call | flops 20912799744 | bytes 36864000 | tf_op jit(solution)/shard_map/mlp_head/pallas_call | solution.py:481
  67.7 3.3 %logprobs.1 = (bf16[8000,512]{1,0:T(8,128)(2,1)}, f32[512]{0:T(512)}, f32[512]{0:T(512)}, f32[512]{0:T(512)}) custom-call(f32[8000,512]{1,0:T(8,128)S(1)} %get-tuple-element.10.lg, f32[3,512]{1,0:T(4,128)S(1)} %get-tuple-element.11.stats), custom_call_target="tpu_custom_call" | custom-call | tf_op jit(solution)/shard_map/logprobs/pallas_call | solution.py:516
